TPU v7x, 256 devices: a whole 4x4x8 slice. The times are simulated.
256 devices in a mesh: seq: 64 (over x, y, z_lo), rep: 4 (over z_hi, core).
Axes of the slice: x: 4, y: 4, z: 8 (z_hi: 2, z_lo: 4; z = z_hi * 4 + z_lo), core: 2. Of those that a mesh axis runs over, the one named last changes fastest.
Arguments:
- prefix_cache: bfloat16 [2, 2, 1024, 32768], P(None, None, 'seq', 'rep'), may hold values from -5 to 5
- queries: bfloat16 [2, 256, 4096], P(None, ('seq', 'rep')), may hold values from -12 to 12
- suffix_cache: bfloat16 [2, 256, 2, 128, 1024], P(None, ('seq', 'rep')), may hold values from -9 to 9
- suffix_lengths: int32 [256], replicated, may hold values from 1 to 128, as said below
- slot_request: int32 [256], P(('seq', 'rep')), may hold values from 0 to 255, each once
Outputs:
- attended: bfloat16 [2, 256, 4096], P(None, ('seq', 'rep'))
Inputs may be any that keep to these rules, and one draw needn't show every extreme that they name: `suffix_lengths`: every request has 1 to 128 suffix tokens; some request has exactly 128. `slot_request`: every request id stands in exactly one slot.
All inputs are finite; a program needn't handle non-finite values.
Results may differ from a plain program's by a relative error of at most 0.005.
Values may be sent and summed in bfloat16 or wider, within the bound.
A program may use at most 64 MiB of HBM per device.

v0:
```python
import jax
import jax.numpy as jnp
from jax import lax
from jax.sharding import PartitionSpec as P

QH = 32
KVH = 8
HD = 128
SUF = 128
GROUP = 4


neg_fill = -1e30


def laid_out(tiles, dim):
    dims = list(tiles.shape[1:])
    dims[dim] *= tiles.shape[0]
    return jnp.moveaxis(tiles, 0, dim).reshape(dims)


def copy_for_each(array, axis):
    copies = jnp.broadcast_to(array, (lax.axis_size(axis), *array.shape))
    return lax.all_to_all(copies, axis, split_axis=0, concat_axis=0, tiled=True)


def collect(array, axis, dim):
    return laid_out(copy_for_each(array, axis), dim)


def sent_together(arrays, axis, split_dim, concat_dim, along):
    widths = [a.shape[along] for a in arrays]
    both = jnp.concatenate(arrays, axis=along)
    whole = lax.all_to_all(both, axis, split_axis=split_dim, concat_axis=concat_dim, tiled=True)
    return tuple(jnp.split(whole, [sum(widths[:k]) for k in range(1, len(widths))], axis=along))


def body(prefix_cache, queries, suffix_cache, suffix_lengths, slot_request):
    layer_total = queries.shape[0]
    own_rows = queries.shape[1]
    score_scale = HD ** (-0.5)
    request_table = jnp.arange(suffix_lengths.shape[0], dtype=jnp.int32)
    lengths = jnp.sum(
        jnp.where(slot_request[:, None] == request_table[None, :], suffix_lengths[None, :], 0),
        axis=1,
    )
    valid_mask = (jnp.arange(SUF, dtype=jnp.int32)[None, :] < lengths[:, None])[:, None, None, :]
    gathered = collect(queries, "seq", 1)
    results = []
    for layer_index in range(layer_total):
        moved_layer = lax.all_to_all(
            prefix_cache[layer_index], "seq", split_axis=2, concat_axis=1, tiled=True
        )
        kv_block = lax.all_gather(moved_layer, "rep", axis=2, tiled=True)
        query_rows = gathered[layer_index]
        row_count = query_rows.shape[0]
        positions = kv_block.shape[2]
        shaped = query_rows.reshape(row_count, KVH, GROUP, HD)
        key_block = kv_block[0].reshape(KVH, HD, positions)
        value_block = kv_block[1].reshape(KVH, HD, positions)
        scores = (
            jnp.einsum("rhgd,hdp->rhgp", shaped, key_block, preferred_element_type=jnp.float32)
            * score_scale
        )
        local_top = jnp.max(scores, axis=3)
        weights = jnp.exp(scores - local_top[..., None]).astype(jnp.bfloat16)
        numerator = jnp.einsum(
            "rhgp,hdp->rhgd", weights, value_block, preferred_element_type=jnp.float32
        ).reshape(row_count, 1, QH * HD)
        denominator = jnp.sum(weights, axis=3, dtype=jnp.float32).reshape(row_count, 1, QH)
        source_tops = local_top.reshape(row_count, 1, QH)
        arrived = sent_together((numerator, denominator, source_tops), "seq", 0, 1, 2)
        own_top = jnp.max(arrived[2], axis=1)
        factor = jnp.exp(arrived[2] - own_top[:, None, :])
        sources = arrived[0].shape[1]
        prefix_num = jnp.sum(
            arrived[0].reshape(own_rows, sources, QH, HD) * factor[..., None], axis=1
        ).reshape(own_rows, QH * HD)
        prefix_den = jnp.sum(arrived[1] * factor, axis=1)
        own_queries = queries[layer_index].reshape(own_rows, KVH, GROUP, HD)
        suffix_keys = suffix_cache[layer_index, :, 0].reshape(own_rows, SUF, KVH, HD)
        suffix_values = suffix_cache[layer_index, :, 1].reshape(own_rows, SUF, KVH, HD)
        suffix_scores = (
            jnp.einsum(
                "rhgd,rshd->rhgs", own_queries, suffix_keys, preferred_element_type=jnp.float32
            )
            * score_scale
        )
        suffix_scores = jnp.where(valid_mask, suffix_scores, neg_fill)
        suffix_top = jnp.max(suffix_scores, axis=3)
        suffix_weights = jnp.where(
            valid_mask, jnp.exp(suffix_scores - suffix_top[..., None]), 0.0
        ).astype(jnp.bfloat16)
        suffix_num = jnp.einsum(
            "rhgs,rshd->rhgd", suffix_weights, suffix_values, preferred_element_type=jnp.float32
        ).reshape(own_rows, QH, HD)
        suffix_den = jnp.sum(suffix_weights, axis=3, dtype=jnp.float32).reshape(own_rows, QH)
        suffix_top = suffix_top.reshape(own_rows, QH)
        both_top = jnp.maximum(own_top, suffix_top)
        prefix_scale = jnp.exp(own_top - both_top)
        suffix_scale = jnp.exp(suffix_top - both_top)
        total_den = prefix_scale * prefix_den + suffix_scale * suffix_den
        mixed = (
            prefix_scale[..., None] * prefix_num.reshape(own_rows, QH, HD)
            + suffix_scale[..., None] * suffix_num
        ) / total_den[..., None]
        results.append(mixed.reshape(own_rows, QH * HD).astype(jnp.bfloat16))
    return jnp.stack(results)


def solution(mesh):
    in_specs = (
        P(None, None, "seq", "rep"),
        P(None, ("seq", "rep"), None),
        P(None, ("seq", "rep"), None, None, None),
        P(),
        P(("seq", "rep")),
    )
    out_specs = P(None, ("seq", "rep"), None)
    return jax.shard_map(body, mesh=mesh, in_specs=in_specs, out_specs=out_specs, check_vma=False)
```

profile of v0, /device:TPU:1, one launch (start us, length us, event | category | flops | bytes accessed | tf_op | source)
XLA Modules:
  0.0 263.0 jit_solution(16606660120096954660)
XLA Ops:
  6.5 1.3 fusion.34
  7.8 6.7 %copy.108 = bf16[1,2,16,8192]{2,1,3,0:T(2,128)(2,1)} copy(bf16[1,2,16,8192]{3,2,1,0:T(8,128)(2,1)S(1)} %get-tuple-element.29) | data formatting | bytes 1048576
  14.5 7.7 %bitcast_bitcast_fusion.1 = bf16[8192,2,16]{2,1,0:T(2,128)(2,1)} fusion(bf16[1,2,16,8192]{2,1,3,0:T(2,128)(2,1)} %copy.108), kind=kLoop, calls=%fused_computation.69 | loop fusion | bytes 1048576
  22.2 12.9 %reshape.519 = bf16[64,2,2048]{2,1,0:T(2,128)(2,1)} reshape(bf16[8192,2,16]{2,1,0:T(2,128)(2,1)} %bitcast_bitcast_fusion.1) | data formatting | bytes 1048576
  35.1 12.5 %all-to-all-start = ((bf16[64,2,2048]{2,1,0:T(2,128)(2,1)}), bf16[64,2,2048]{2,1,0:T(2,128)(2,1)S(1)}, u32[]{:S(2)}, u32[]{:S(2)}) async-start(bf16[64,2,2048]{2,1,0:T(2,128)(2,1)} %reshape.519), calls=%async_computation | async-start | bytes 1048576 | tf_op jit(solution)/shard_map/all_to_all | solution.py:51
  47.7 6.7 %copy.111 = bf16[1,2,16,8192]{2,1,3,0:T(2,128)(2,1)} copy(bf16[1,2,16,8192]{3,2,1,0:T(8,128)(2,1)S(1)} %get-tuple-element.30) | data formatting | bytes 1048576
  54.4 10.7 %all-to-all-done = bf16[64,2,2048]{2,1,0:T(2,128)(2,1)S(1)} async-done(((bf16[64,2,2048]{2,1,0:T(2,128)(2,1)}), bf16[64,2,2048]{2,1,0:T(2,128)(2,1)S(1)}, u32[]{:S(2)}, u32[]{:S(2)}) %all-to-all-start) | async-done | bytes 524320 | tf_op jit(solution)/shard_map/all_to_all | solution.py:51
  65.1 4.1 %reshape.520 = bf16[8192,2,16]{2,1,0:T(2,128)(2,1)} reshape(bf16[64,2,2048]{2,1,0:T(2,128)(2,1)S(1)} %all-to-all-done) | data formatting | bytes 1048576
  69.2 8.8 %copy.77 = bf16[2,64,16,128]{3,2,1,0:T(8,128)(2,1)} copy(bf16[2,64,16,128]{2,0,3,1:T(2,128)(2,1)} %bitcast.106) | data formatting | bytes 1048576 | tf_op jit(solution)/shard_map/all_to_all | solution.py:51
  78.1 7.7 %bitcast_bitcast_fusion = bf16[8192,2,16]{2,1,0:T(2,128)(2,1)} fusion(bf16[1,2,16,8192]{2,1,3,0:T(2,128)(2,1)} %copy.111), kind=kLoop, calls=%fused_computation.68 | loop fusion | bytes 1048576
  85.8 12.3 %reshape.517 = bf16[64,2,2048]{2,1,0:T(2,128)(2,1)S(1)} reshape(bf16[8192,2,16]{2,1,0:T(2,128)(2,1)} %bitcast_bitcast_fusion) | data formatting | bytes 1048576
  98.1 32.6 %all_to_all.65 = bf16[64,2,2048]{2,1,0:T(2,128)(2,1)S(1)} all-to-all(bf16[64,2,2048]{2,1,0:T(2,128)(2,1)S(1)} %reshape.517), channel_id=1, replica_groups=mesh['seq'=64,'rep'=4] {'seq'}, dimensions={0} | all-to-all | bytes 1048576 | tf_op jit(solution)/shard_map/all_to_all | solution.py:51
  130.7 2.1 broadcast_in_dim.53
  132.8 4.7 %all-to-all-start.1 = ((bf16[64,2,1,4096]{3,1,2,0:T(2,128)(2,1)}), bf16[64,2,1,4096]{3,1,2,0:T(2,128)(2,1)S(1)}, u32[]{:S(2)}, u32[]{:S(2)}) async-start(bf16[64,2,1,4096]{3,1,2,0:T(2,128)(2,1)} %broadcast_in_dim.53), calls=%async_computation.1 | async-start | bytes 2097152 | tf_op jit(solution)/shard_map/all_to_all | solution.py:24
  137.5 4.1 %reshape.518 = bf16[8192,2,16]{2,1,0:T(2,128)(2,1)} reshape(bf16[64,2,2048]{2,1,0:T(2,128)(2,1)S(1)} %all_to_all.65) | data formatting | bytes 1048576
  141.7 8.8 %copy.89 = bf16[2,64,16,128]{3,2,1,0:T(8,128)(2,1)} copy(bf16[2,64,16,128]{2,0,3,1:T(2,128)(2,1)} %bitcast.107) | data formatting | bytes 1048576 | tf_op jit(solution)/shard_map/all_to_all | solution.py:51
  150.6 15.4 %all-to-all-done.1 = bf16[64,2,1,4096]{3,1,2,0:T(2,128)(2,1)S(1)} async-done(((bf16[64,2,1,4096]{3,1,2,0:T(2,128)(2,1)}), bf16[64,2,1,4096]{3,1,2,0:T(2,128)(2,1)S(1)}, u32[]{:S(2)}, u32[]{:S(2)}) %all-to-all-start.1) | async-done | bytes 1048608 | tf_op jit(solution)/shard_map/all_to_all | solution.py:24
  165.9 5.4 %slice_reduce_fusion.1 = (bf16[64,4096]{1,0:T(8,128)(2,1)S(1)}, bf16[64,4096]{1,0:T(8,128)(2,1)S(1)}) fusion(bf16[2,64,1,4096]{3,0,2,1:T(2,128)(2,1)S(1)} %bitcast.108), kind=kLoop, calls=%fused_computation.19 | loop fusion | bytes 2097152 | tf_op jit(solution)/shard_map/slice | solution.py:55
  171.8 1.7 fusion.31
  174.3 1.9 copy-done
  178.6 3.2 %convert_reduce_fusion.1 = f32[64,8,4]{0,2,1:T(4,128)S(1)} fusion(f32[64,8,4]{0,2,1:T(4,128)S(1)} %get-tuple-element.37, f32[8,512,64,4]{1,2,3,0:T(8,128)} %copy-done), kind=kLoop, calls=%fused_computation.9 | loop fusion | flops 5240832 | bytes 4210688 | tf_op jit(solution)/shard_map/reduce_sum | solution.py:70
  182.1 2.1 copy.82
  184.2 5.3 %all-to-all-start.2 = ((f32[64,1,4160]{2,1,0:T(1,128)}), f32[64,1,4160]{2,1,0:T(1,128)S(1)}, u32[]{:S(2)}, u32[]{:S(2)}) async-start(f32[64,1,4160]{2,1,0:T(1,128)} %copy.82), calls=%async_computation.2 | async-start | bytes 2162688 | tf_op jit(solution)/shard_map/all_to_all | solution.py:34
  189.8 5.3 %all-gather.5.cloned.1.call-done = bf16[2,1024,512]{2,1,0:T(8,128)(2,1)} async-done(((bf16[2,1024,128]{2,1,0:T(8,128)(2,1)}), bf16[2,1024,512]{2,1,0:T(8,128)(2,1)}) %all-gather.5.cloned.1.call-update) | async-done | bytes 2097168 | tf_op jit(solution)/shard_map/all_gather | solution.py:54
  195.1 1.7 fusion.32
  197.6 1.9 copy-done.1
  199.5 1.2 convolution_bitcast_fusion
  201.9 3.2 %convert_reduce_fusion = f32[64,8,4]{0,2,1:T(4,128)S(1)} fusion(f32[64,8,4]{0,2,1:T(4,128)S(1)} %get-tuple-element.35, f32[8,512,64,4]{1,2,3,0:T(8,128)} %copy-done.1), kind=kLoop, calls=%fused_computation.8 | loop fusion | flops 5240832 | bytes 4210688 | tf_op jit(solution)/shard_map/reduce_sum | solution.py:70
  205.5 2.1 copy.94
  207.6 11.8 %all-to-all-done.2 = f32[64,1,4160]{2,1,0:T(1,128)S(1)} async-done(((f32[64,1,4160]{2,1,0:T(1,128)}), f32[64,1,4160]{2,1,0:T(1,128)S(1)}, u32[]{:S(2)}, u32[]{:S(2)}) %all-to-all-start.2) | async-done | bytes 1064992 | tf_op jit(solution)/shard_map/all_to_all | solution.py:34
  219.4 4.7 %all-to-all-start.4 = ((f32[64,1,4160]{2,1,0:T(1,128)}), f32[64,1,4160]{2,1,0:T(1,128)S(1)}, u32[]{:S(2)}, u32[]{:S(2)}) async-start(f32[64,1,4160]{2,1,0:T(1,128)} %copy.94), calls=%async_computation.4 | async-start | bytes 2162688 | tf_op jit(solution)/shard_map/all_to_all | solution.py:34
  234.1 19.1 %all-to-all-done.4 = f32[64,1,4160]{2,1,0:T(1,128)S(1)} async-done(((f32[64,1,4160]{2,1,0:T(1,128)}), f32[64,1,4160]{2,1,0:T(1,128)S(1)}, u32[]{:S(2)}, u32[]{:S(2)}) %all-to-all-start.4) | async-done | bytes 1064992 | tf_op jit(solution)/shard_map/all_to_all | solution.py:34
  (63 shorter events, 19.0 us)
Async XLA Ops:
  35.1 30.0 %all-to-all-start = ((bf16[64,2,2048]{2,1,0:T(2,128)(2,1)}), bf16[64,2,2048]{2,1,0:T(2,128)(2,1)S(1)}, u32[]{:S(2)}, u32[]{:S(2)}) async-start(bf16[64,2,2048]{2,1,0:T(2,128)(2,1)} %reshape.519), calls=%async_computation | async-start | bytes 1048576 | tf_op jit(solution)/shard_map/all_to_all | solution.py:51
  47.7 124.1 %all-gather.3.cloned.1.call-start = ((), (), s32[]{:S(2)}) async-start(), calls=%async_computation.5 | async-start | bytes 2621440 | tf_op jit(solution)/shard_map/all_gather | solution.py:54
  85.8 44.9 %copy-start.3 = (bf16[2,1,4096]{2,0,1:T(2,128)(2,1)S(1)}, bf16[2,1,4096]{2,0,1:T(2,128)(2,1)}, u32[]{:S(2)}) copy-start(bf16[2,1,4096]{2,0,1:T(2,128)(2,1)} %param.6) | copy-start | bytes 49156
  132.8 33.1 %all-to-all-start.1 = ((bf16[64,2,1,4096]{3,1,2,0:T(2,128)(2,1)}), bf16[64,2,1,4096]{3,1,2,0:T(2,128)(2,1)S(1)}, u32[]{:S(2)}, u32[]{:S(2)}) async-start(bf16[64,2,1,4096]{3,1,2,0:T(2,128)(2,1)} %broadcast_in_dim.53), calls=%async_computation.1 | async-start | bytes 2097152 | tf_op jit(solution)/shard_map/all_to_all | solution.py:24
  137.5 57.6 %all-gather.5.cloned.1.call-start = ((), (), s32[]{:S(2)}) async-start(), calls=%async_computation.6 | async-start | bytes 2621440 | tf_op jit(solution)/shard_map/all_gather | solution.py:54
  174.2 1.9 copy-start
  184.2 35.2 %all-to-all-start.2 = ((f32[64,1,4160]{2,1,0:T(1,128)}), f32[64,1,4160]{2,1,0:T(1,128)S(1)}, u32[]{:S(2)}, u32[]{:S(2)}) async-start(f32[64,1,4160]{2,1,0:T(1,128)} %copy.82), calls=%async_computation.2 | async-start | bytes 2162688 | tf_op jit(solution)/shard_map/all_to_all | solution.py:34
  197.6 1.9 copy-start.1
  205.4 18.6 %copy-start.2 = (bf16[2,1,2,128,1024]{4,3,2,1,0:T(8,128)(2,1)S(1)}, bf16[2,1,2,128,1024]{4,3,2,1,0:T(8,128)(2,1)}, u32[]{:S(2)}) copy-start(bf16[2,1,2,128,1024]{4,3,2,1,0:T(8,128)(2,1)} %param.7) | copy-start | bytes 3145732
  205.4 22.4 %copy-start.4 = (s32[256]{0:T(256)S(1)}, s32[256]{0:T(256)}, u32[]{:S(2)}) copy-start(s32[256]{0:T(256)} %param.8) | copy-start | bytes 3076
  219.4 33.8 %all-to-all-start.4 = ((f32[64,1,4160]{2,1,0:T(1,128)}), f32[64,1,4160]{2,1,0:T(1,128)S(1)}, u32[]{:S(2)}, u32[]{:S(2)}) async-start(f32[64,1,4160]{2,1,0:T(1,128)} %copy.94), calls=%async_computation.4 | async-start | bytes 2162688 | tf_op jit(solution)/shard_map/all_to_all | solution.py:34
Sparse Core Ops, SparseCore 0:
  78.2 37.6 all-gather.2
  150.7 44.3 all-gather.4
where the time goes:
time: 264 us; the launch traced here: 263 us
  local copies, waits for them, and re-layouts  110 us (42%)
  waiting for transfers between devices  62.3 us (24%)
  blocking collectives  32.6 us (12%)
  starting transfers between devices  27.2 us (10%)
  between operations  14.3 us (5%)
  other arithmetic  11.7 us (4%)
  matrix products  5.05 us (2%)
    unnamed x22, local copies, waits for them, and re-layouts  69.7 us
    all_to_all x1, blocking collectives, body(): lax.all_to_all(prefix_cache[layer_index], 'seq', split_axis=2, concat_axi...  32.6 us
    all_to_all x2, waiting for transfers between devices, sent_together(): lax.all_to_all(both, axis, split_axis=split_dim, concat_axis=concat_dim,...  30.9 us
    all_to_all x2, local copies, waits for them, and re-layouts, body(): lax.all_to_all(prefix_cache[layer_index], 'seq', split_axis=2, concat_axi...  17.7 us
    all_to_all x1, waiting for transfers between devices, copy_for_each(): return lax.all_to_all(copies, axis, split_axis=0, concat_axis=0, tiled=True)  15.4 us
    all_to_all x1, starting transfers between devices, body(): lax.all_to_all(prefix_cache[layer_index], 'seq', split_axis=2, concat_axi...  12.5 us
    all_to_all x1, waiting for transfers between devices, body(): lax.all_to_all(prefix_cache[layer_index], 'seq', split_axis=2, concat_axi...  10.7 us
    all_to_all x2, starting transfers between devices, sent_together(): lax.all_to_all(both, axis, split_axis=split_dim, concat_axis=concat_dim,...  9.91 us
  transfers between devices with their start and end apart: 6, of which 5 were waited for; matrix products, arithmetic and copies ran while one was open for 30% of the time, Pallas kernels for 0%

commit v1 on v0

v1 whole, which is shorter than its diff:
```python
import functools
import math

import jax
import jax.numpy as jnp
from jax import lax
from jax.experimental import pallas as pl
from jax.experimental.pallas import tpu as pltpu
from jax.sharding import PartitionSpec as P

QH = 32
KVH = 8
HD = 128
SUF = 128
GROUP = 4
NEG = -1e30
SCALE2 = HD ** -0.5 * math.log2(math.e)
POS = 1024
NT = (((1,), (1,)), ((), ()))
NN = (((1,), (0,)), ((), ()))
MESH = pl.DeviceIdType.MESH


def dot(a, b, dims):
    return lax.dot_general(a, b, dims, preferred_element_type=jnp.float32)


def kernel(
    prefix, qmsg, suffix, lengths, slot, out,
    stage, kown, koth, suf, qa, qall, wbuf, lrep, rden, sbuf_o, sbuf_l,
    osend, lsend, orecv, lrecv, fsend, frecv,
    loc_sem, a_s, a_r, kv_s, kv_r, b_s, b_r, y_sem, f_s, f_r, c_s, c_r, l_s, l_r, d_s, d_r,
):
    seq = lax.axis_index("seq")
    rep = lax.axis_index("rep")
    x, y, zl = seq // 16, (seq // 4) % 4, seq % 4
    yh, yl = y // 2, y % 2
    zh, c = rep // 2, rep % 2
    z = zh * 4 + zl
    head = x * 2 + yh
    part = yl * 4 + zl
    place = yl * 8 + z

    def at(head_to, yl_to, z_to, c_to):
        x_to, yh_to = head_to // 2, head_to % 2
        return ((x_to * 4 + yh_to * 2 + yl_to) * 4 + z_to % 4, (z_to // 4) * 2 + c_to)

    def remote(src, dst, s, r, dev):
        return pltpu.make_async_remote_copy(
            src_ref=src, dst_ref=dst, send_sem=s, recv_sem=r, device_id=dev, device_id_type=MESH)

    loads = [pltpu.make_async_copy(prefix.at[l, k], stage.at[l, k], loc_sem.at[l * 2 + k])
             for l in range(2) for k in range(2)]
    owns = [pltpu.make_async_copy(
        prefix.at[l, k, :, pl.ds(pl.multiple_of(part * POS, POS), POS)],
        kown.at[l, k, part], loc_sem.at[4 + l * 2 + k]) for l in range(2) for k in range(2)]
    load_suf = pltpu.make_async_copy(suffix, suf, loc_sem.at[8])
    for cp in loads + owns:
        cp.start()
    load_suf.start()

    barrier = pltpu.get_barrier_semaphore()
    peers = []
    for k in range(1, 8):
        peers.append(at((head + k) % 8, yl, z, c))
    for k in range(1, 16):
        to = (place + k) % 16
        peers.append(at(head, to // 8, to % 8, c))
    other = at(head, yl, z, 1 - c)
    peers.append(other)
    for dev in peers:
        pl.semaphore_signal(barrier, inc=1, device_id=dev, device_id_type=MESH)
    pl.semaphore_wait(barrier, len(peers))

    def a_copy(k):
        to = (head + k) % 8
        return remote(qmsg.at[to], qa.at[head], a_s.at[k], a_r.at[head], at(to, yl, z, c))

    for k in range(1, 8):
        a_copy(k).start()
    qa[head] = qmsg[head]

    steps = [(2, 0), (2, 1), (1, 0), (1, 1), (3, 0), (3, 1), (0, 1)]

    def kv_copy(l, k, i):
        dz, dy = steps[i]
        yl_to, zl_to = (yl + dy) % 2, (zl + dz) % 4
        to = yl_to * 4 + zl_to
        return remote(
            stage.at[l, k, :, pl.ds(pl.multiple_of(to * POS, POS), POS)],
            kown.at[l, k, part], kv_s.at[l * 2 + k, i], kv_r.at[l * 2 + k, part],
            at(head, yl_to, zh * 4 + zl_to, c))

    def kv_send(l, k):
        loads[l * 2 + k].wait()
        for i in range(7):
            kv_copy(l, k, i).start()

    def kv_wait(l, k):
        owns[l * 2 + k].wait()
        for i in range(1, 8):
            src = (part + i) % 8
            remote(kown.at[l, k, src], kown.at[l, k, src], kv_s.at[l * 2 + k, 0],
                   kv_r.at[l * 2 + k, src], other).wait_recv()

    def forward(l, k):
        return remote(kown.at[l, k], koth.at[l, k], f_s.at[l * 2 + k], f_r.at[l * 2 + k], other)

    kv_send(0, 0)

    for k in range(1, 8):
        src = (head + k) % 8
        remote(qa.at[src], qa.at[src], a_s.at[0], a_r.at[src], other).wait_recv()
    mine = jnp.swapaxes(qa[...].astype(jnp.float32), 0, 1).reshape(64, HD)
    qall[place] = mine.astype(jnp.bfloat16)

    def b_copy(k):
        return remote(qall.at[place], qall.at[place], b_s.at[k], b_r.at[z],
                      at(head, yl, (z + k) % 8, c))

    load_suf.wait()
    count = lengths[slot[0]]
    row = lax.broadcasted_iota(jnp.int32, (8, HD), 0)
    lane = lax.broadcasted_iota(jnp.int32, (8, HD), 1)
    valid = lane < count

    def suffix_head(h):
        cols = slice(h * HD, (h + 1) * HD)
        q = qmsg[h]
        s0 = dot(q, suf[0, 0, 0, :, cols], NT)
        s1 = dot(q, suf[1, 0, 0, :, cols], NT)
        s = jnp.where(valid, jnp.where(row < GROUP, s0, s1) * SCALE2, NEG)
        top = jnp.max(s, axis=1, keepdims=True)
        w = jnp.where(valid, jnp.exp2(s - top), 0.0).astype(jnp.bfloat16)
        den = jnp.sum(w.astype(jnp.float32), axis=1, keepdims=True)
        n0 = dot(w, suf[0, 0, 1, :, cols], NN)
        n1 = dot(w, suf[1, 0, 1, :, cols], NN)
        sbuf_o[h] = jnp.where(row < GROUP, n0, n1) / den
        sbuf_l[h] = jnp.broadcast_to(top + jnp.log2(den), (8, HD))

    suffix_head(0)
    for k in (4, 3, 5, 2, 6, 1, 7):
        b_copy(k).start()
    kv_send(0, 1)
    kv_send(1, 0)
    kv_send(1, 1)
    for h in range(1, KVH):
        suffix_head(h)

    for k in range(1, 8):
        src = yl * 8 + (z + k) % 8
        remote(qall.at[src], qall.at[src], b_s.at[0], b_r.at[(z + k) % 8], other).wait_recv()
    half = pl.ds(yl * 8, 8)
    rest = pl.ds((1 - yl) * 8, 8)
    y_copy = remote(qall.at[half], qall.at[half], y_sem.at[0], y_sem.at[1], at(head, 1 - yl, z, c))
    y_copy.start()
    kv_wait(0, 0)
    forward(0, 0).start()
    remote(qall.at[rest], qall.at[rest], y_sem.at[0], y_sem.at[1], other).wait_recv()

    def weights(l):
        remote(koth.at[l, 0], koth.at[l, 0], f_s.at[l * 2], f_r.at[l * 2], other).wait_recv()

        def rows(i, carry):
            q = qall[pl.ds(i * 4, 4), l * 32:(l + 1) * 32, :].reshape(128, HD)
            at_rows = pl.ds(pl.multiple_of(i * 128, 128), 128)
            sa = dot(q, kown[l, 0].reshape(HD, POS), NN) * SCALE2
            sb = dot(q, koth[l, 0].reshape(HD, POS), NN) * SCALE2
            top = jnp.maximum(jnp.max(sa, axis=1, keepdims=True), jnp.max(sb, axis=1, keepdims=True))
            wa = jnp.exp2(sa - top).astype(jnp.bfloat16)
            wb = jnp.exp2(sb - top).astype(jnp.bfloat16)
            den = jnp.sum(wa.astype(jnp.float32) + wb.astype(jnp.float32), axis=1, keepdims=True)
            wbuf[0, at_rows, :] = wa
            wbuf[1, at_rows, :] = wb
            lrep[at_rows, :] = jnp.broadcast_to(top + jnp.log2(den), (128, HD))
            rden[at_rows, :] = jnp.broadcast_to(1.0 / den, (128, HD))
            return carry

        lax.fori_loop(0, 4, rows, 0)

    def values(l):
        row32 = lax.broadcasted_iota(jnp.int32, (4, 32, HD), 1)
        lane32 = lax.broadcasted_iota(jnp.int32, (4, 32, HD), 2)

        remote(koth.at[l, 1], koth.at[l, 1], f_s.at[l * 2 + 1], f_r.at[l * 2 + 1], other).wait_recv()

        def rows(i, carry):
            at_rows = pl.ds(pl.multiple_of(i * 128, 128), 128)
            o = dot(wbuf[0, at_rows, :], kown[l, 1].reshape(HD, POS), NT)
            o = o + dot(wbuf[1, at_rows, :], koth[l, 1].reshape(HD, POS), NT)
            o = o * rden[at_rows, :]
            osend[l, pl.ds(i * 4, 4)] = o.astype(jnp.bfloat16).reshape(4, 32, HD)
            lx = lrep[at_rows, :].reshape(4, 32, HD)
            lsend[l, pl.ds(i * 4, 4)] = jnp.sum(
                jnp.where(row32 == lane32, lx, 0.0), axis=1, keepdims=True)
            return carry

        lax.fori_loop(0, 4, rows, 0)
        for k in range(1, 16):
            to = (place + k) % 16
            dev = at(head, to // 8, to % 8, c)
            remote(osend.at[l, to], orecv.at[l, place], c_s.at[l, k], c_r.at[l, place], dev).start()
            remote(lsend.at[l, to], lrecv.at[l, place], l_s.at[l, k], l_r.at[l, place], dev).start()
        orecv[l, place] = osend[l, place]
        lrecv[l, place] = lsend[l, place]

    weights(0)
    kv_wait(0, 1)
    forward(0, 1).start()
    values(0)
    kv_wait(1, 0)
    forward(1, 0).start()
    weights(1)
    kv_wait(1, 1)
    forward(1, 1).start()
    values(1)

    def combine(l):
        for k in range(1, 16):
            src = (place + k) % 16
            remote(orecv.at[l, src], orecv.at[l, src], c_s.at[l, 0], c_r.at[l, src], other).wait_recv()
            remote(lrecv.at[l, src], lrecv.at[l, src], l_s.at[l, 0], l_r.at[l, src], other).wait_recv()
        ls = lrecv[l].reshape(16, HD)
        top = jnp.max(ls, axis=0, keepdims=True)
        w = jnp.exp2(ls - top)
        den = jnp.sum(w, axis=0, keepdims=True)
        w = w / den
        total = jnp.broadcast_to(top + jnp.log2(den), (112, HD))
        cols = jnp.concatenate([w, total], axis=0).T
        o = jnp.zeros((32, HD), jnp.float32)
        for s in range(16):
            o = o + orecv[l, s].astype(jnp.float32) * cols[:32, s:s + 1]
        lall = jnp.broadcast_to(cols[:32, 16:17], (32, HD))
        both = jnp.concatenate([o.reshape(4, 8, HD), lall.reshape(4, 8, HD)], axis=0)
        fsend[l] = jnp.swapaxes(both, 0, 1)
        for k in range(1, 8):
            to = (head + k) % 8
            remote(fsend.at[l, to], frecv.at[l, head], d_s.at[l, k], d_r.at[l, head],
                   at(to, yl, z, c)).start()
        frecv[l, head] = fsend[l, head]

    def finish(l):
        for k in range(1, 8):
            src = (head + k) % 8
            remote(frecv.at[l, src], frecv.at[l, src], d_s.at[l, 0], d_r.at[l, src], other).wait_recv()
        got = frecv[l]
        o_p, l_p = got[:, :GROUP, :], got[:, GROUP:, :]
        o_s = sbuf_o[...][:, l * GROUP:(l + 1) * GROUP, :]
        l_s_ = sbuf_l[...][:, l * GROUP:(l + 1) * GROUP, :]
        top = jnp.maximum(l_p, l_s_)
        a = jnp.exp2(l_p - top)
        b = jnp.exp2(l_s_ - top)
        out[l] = ((a * o_p + b * o_s) / (a + b)).astype(jnp.bfloat16)

    combine(0)
    combine(1)
    finish(0)
    finish(1)

    for k in range(1, 8):
        a_copy(k).wait_send()
        b_copy(k).wait_send()
    y_copy.wait_send()
    for l in range(2):
        for k in range(2):
            for i in range(7):
                kv_copy(l, k, i).wait_send()
            forward(l, k).wait_send()
        for k in range(1, 16):
            remote(osend.at[l, 0], orecv.at[l, 0], c_s.at[l, k], c_r.at[l, 0], other).wait_send()
            remote(lsend.at[l, 0], lrecv.at[l, 0], l_s.at[l, k], l_r.at[l, 0], other).wait_send()
        for k in range(1, 8):
            remote(fsend.at[l, 0], frecv.at[l, 0], d_s.at[l, k], d_r.at[l, 0], other).wait_send()


def body(prefix_cache, queries, suffix_cache, suffix_lengths, slot_request):
    bf, f32 = jnp.bfloat16, jnp.float32
    qmsg = queries.reshape(2, KVH, GROUP, HD).transpose(1, 0, 2, 3).reshape(KVH, 2 * GROUP, HD)
    dma = pltpu.SemaphoreType.DMA
    any_space = pl.BlockSpec(memory_space=pl.ANY)
    out = pl.pallas_call(
        kernel,
        out_shape=jax.ShapeDtypeStruct((2, KVH, GROUP, HD), bf),
        in_specs=[
            any_space,
            pl.BlockSpec(memory_space=pltpu.VMEM),
            any_space,
            pl.BlockSpec(memory_space=pltpu.SMEM),
            pl.BlockSpec(memory_space=pltpu.SMEM),
        ],
        out_specs=pl.BlockSpec(memory_space=pltpu.VMEM),
        scratch_shapes=[
            pltpu.VMEM((2, 2, 16, 8192), bf),
            pltpu.VMEM((2, 2, 8, 16, POS), bf),
            pltpu.VMEM((2, 2, 8, 16, POS), bf),
            pltpu.VMEM((2, 1, 2, SUF, KVH * HD), bf),
            pltpu.VMEM((8, 8, HD), bf),
            pltpu.VMEM((16, 64, HD), bf),
            pltpu.VMEM((2, 512, POS), bf),
            pltpu.VMEM((512, HD), f32),
            pltpu.VMEM((512, HD), f32),
            pltpu.VMEM((KVH, 8, HD), f32),
            pltpu.VMEM((KVH, 8, HD), f32),
            pltpu.VMEM((2, 16, 32, HD), bf),
            pltpu.VMEM((2, 16, 1, HD), f32),
            pltpu.VMEM((2, 16, 32, HD), bf),
            pltpu.VMEM((2, 16, 1, HD), f32),
            pltpu.VMEM((2, 8, 8, HD), f32),
            pltpu.VMEM((2, 8, 8, HD), f32),
            dma((9,)),
            dma((8,)), dma((8,)),
            dma((4, 8)), dma((4, 8)),
            dma((8,)), dma((8,)),
            dma((2,)),
            dma((4,)), dma((4,)),
            dma((2, 16)), dma((2, 16)),
            dma((2, 16)), dma((2, 16)),
            dma((2, 8)), dma((2, 8)),
        ],
        compiler_params=pltpu.CompilerParams(collective_id=0, has_side_effects=True),
        name="attend",
    )(prefix_cache, qmsg, suffix_cache, suffix_lengths, slot_request)
    return out.reshape(2, 1, QH * HD)


def solution(mesh):
    in_specs = (
        P(None, None, "seq", "rep"),
        P(None, ("seq", "rep"), None),
        P(None, ("seq", "rep"), None, None, None),
        P(),
        P(("seq", "rep")),
    )
    out_specs = P(None, ("seq", "rep"), None)
    return jax.shard_map(body, mesh=mesh, in_specs=in_specs, out_specs=out_specs, check_vma=False)
```

time: 264 us -> 60.2 us (0.23)
  local copies, waits for them, and re-layouts: 110 us -> 2.69 us
  waiting for transfers between devices: 62.3 us -> 0 us
  Pallas kernels: 0 us -> 56.5 us
  blocking collectives: 32.6 us -> 0 us
  starting transfers between devices: 27.2 us -> 0 us
  between operations: 14.3 us -> 0.66 us
  other arithmetic: 11.7 us -> 0 us
  matrix products: 5.05 us -> 0 us
    unnamed x22 -> x0, local copies, waits for them, and re-layouts: 69.7 us -> none
    all_to_all x4 -> x0, waiting for transfers between devices: 57 us -> none  [the longest x2 30.9 us: sent_together(): lax.all_to_all(both, axis, split_axis=split_dim, concat_axis=concat_dim,...]
    pallas_call x0 -> x1, Pallas kernels: none -> 56.5 us  [body(): pl.pallas_call(kernel, out_shape=jax.ShapeDtypeStruct((2, KVH, GROUP, HD)...]
    all_to_all x1 -> x0, blocking collectives: 32.6 us -> none  [body(): lax.all_to_all(prefix_cache[layer_index], 'seq', split_axis=2, concat_axi...]
    all_to_all x4 -> x0, starting transfers between devices: 27.1 us -> none  [the longest x1 12.5 us: body(): lax.all_to_all(prefix_cache[layer_index], 'seq', split_axis=2, concat_axi...]
    all_to_all x2 -> x0, local copies, waits for them, and re-layouts: 17.7 us -> none  [body(): lax.all_to_all(prefix_cache[layer_index], 'seq', split_axis=2, concat_axi...]
    slice x6 -> x0, local copies, waits for them, and re-layouts: 11.1 us -> none  [the longest x1 5.42 us: body(): query_rows = gathered[layer_index]]
    reduce_sum x8 -> x0, other arithmetic: 9.94 us -> none  [the longest x2 6.43 us: body(): jnp.sum(weights, axis=3, dtype=jnp.float32).reshape(row_count, 1, QH)]
  transfers between devices with their start and end apart: 6 -> 0, of which waited for: 5 -> 0; matrix products, arithmetic and copies ran while one was open for 30% -> 0% of each run, Pallas kernels for 0% -> 0%
where the time goes in v1:
time: 60.2 us; the launch traced here: 59.8 us
  Pallas kernels  56.5 us (94%)
  local copies, waits for them, and re-layouts  2.69 us (4%)
  between operations  0.66 us (1%)
    pallas_call x1, Pallas kernels, body(): pl.pallas_call(kernel, out_shape=jax.ShapeDtypeStruct((2, KVH, GROUP, HD)...  56.5 us
    reshape x2, local copies, waits for them, and re-layouts, body(): queries.reshape(2, KVH, GROUP, HD).transpose(1, 0, 2, 3)  1.35 us
    reshape x1, local copies, waits for them, and re-layouts, body(): return out.reshape(2, 1, QH * HD)  1.33 us

profile of v1, /device:TPU:1, one launch (start us, length us, event | category | flops | bytes accessed | tf_op | source)
XLA Modules:
  0.0 59.8 jit_solution(5289672456484497698)
XLA Ops:
  0.7 0.7 %reshape.9 = bf16[2,8,4,128]{3,2,1,0:T(4,128)(2,1)S(1)} reshape(bf16[2,1,4096]{2,0,1:T(2,128)(2,1)} %param.6) | data formatting | bytes 32768 | tf_op jit(solution)/shard_map/reshape | solution.py:278
  1.4 0.6 %copy.6 = bf16[2,8,4,128]{3,2,0,1:T(4,128)(2,1)} copy(bf16[2,8,4,128]{3,2,1,0:T(4,128)(2,1)S(1)} %reshape.9) | data formatting | bytes 32768 | tf_op jit(solution)/shard_map/reshape | solution.py:278
  2.0 56.5 %attend.1 = bf16[2,8,4,128]{3,2,1,0:T(4,128)(2,1)} custom-call(bf16[2,2,16,8192]{3,2,1,0:T(8,128)(2,1)} %prefix.1, bf16[8,8,128]{2,1,0:T(8,128)(2,1)} %bitcast.5, bf16[2,1,2,128,1024]{4,3,2,1,0:T(8,128)(2,1)} %suffix.1, s32[256]{0:T(256)} %lengths.1, s32[1]{0:T(128)S(6)} %copy.7.slot), custom_call_target="tpu_custom_call" | custom-call | tf_op jit(solution)/shard_map/attend/pallas_call | solution.py:281
  58.5 1.3 %reshape.11 = bf16[2,1,4096]{2,0,1:T(2,128)(2,1)} reshape(bf16[2,8,4,128]{3,2,1,0:T(4,128)(2,1)} %attend.1) | data formatting | bytes 32768 | tf_op jit(solution)/shard_map/reshape | solution.py:323

commit v2 on v1

v2 whole, which is shorter than its diff:
```python
import math

import jax
import jax.numpy as jnp
from jax import lax
from jax.experimental import pallas as pl
from jax.experimental.pallas import tpu as pltpu
from jax.sharding import PartitionSpec as P

QH = 32
KVH = 8
HD = 128
SUF = 128
GROUP = 4
NEG = -1e30
SCALE2 = HD ** -0.5 * math.log2(math.e)
POS = 1024
NT = (((1,), (1,)), ((), ()))
NN = (((1,), (0,)), ((), ()))
MESH = pl.DeviceIdType.MESH


def dot(a, b, dims):
    return lax.dot_general(a, b, dims, preferred_element_type=jnp.float32)


def kernel(
    prefix, queries, suffix, lengths, slot, out,
    stage, kown, koth, suf, qraw, qmsg, qa, qall, wbuf, rden, oacc, sbuf_o, sbuf_l,
    osend, orecv, lsend, lrecv, gsend, grecv, fsend, frecv,
    loc_sem, a_sem, b_sem, y_sem, kv_s, kv_r, v1_r, f_s, f_r, c_s, c_r, l_sem, g_sem, d_s, d_r,
):
    f32, bf16 = jnp.float32, jnp.bfloat16
    seq = lax.axis_index("seq")
    rep = lax.axis_index("rep")
    x, y, zl = seq // 16, (seq // 4) % 4, seq % 4
    yh, yl = y // 2, y % 2
    zh, c = rep // 2, rep % 2
    z = zh * 4 + zl
    head = x * 2 + yh
    part = yl * 4 + zl
    spot = head * 2 + yl

    def at(head_to, yl_to, z_to, c_to):
        x_to, yh_to = head_to // 2, head_to % 2
        return ((x_to * 4 + yh_to * 2 + yl_to) * 4 + z_to % 4, (z_to // 4) * 2 + c_to)

    other = at(head, yl, z, 1 - c)

    def remote(src, dst, s, r, dev=other):
        return pltpu.make_async_remote_copy(
            src_ref=src, dst_ref=dst, send_sem=s, recv_sem=r, device_id=dev, device_id_type=MESH)

    load_q = pltpu.make_async_copy(queries, qraw, loc_sem.at[9])
    load_q.start()
    order = ((0, 0), (1, 0), (0, 1), (1, 1))
    loads = {(l, k): pltpu.make_async_copy(prefix.at[l, k], stage.at[l, k], loc_sem.at[l * 2 + k])
             for l, k in order}
    owns = {(l, k): pltpu.make_async_copy(
        prefix.at[l, k, :, pl.ds(pl.multiple_of(part * POS, POS), POS)],
        kown.at[l, k, part], loc_sem.at[4 + l * 2 + k]) for l, k in order}
    load_suf = pltpu.make_async_copy(suffix, suf, loc_sem.at[8])
    loads[0, 0].start()
    load_suf.start()

    barrier = pltpu.get_barrier_semaphore()
    peers = [other]
    for k in range(1, 16):
        to = (spot + k) % 16
        peers.append(at(to // 2, to % 2, z, c))
    for k in range(1, 8):
        peers.append(at(head, yl, (z + k) % 8, c))
    for k in range(1, 4):
        peers.append(at(head, 1 - yl, zh * 4 + (zl + k) % 4, c))
    for dev in peers:
        pl.semaphore_signal(barrier, inc=1, device_id=dev, device_id_type=MESH)
    for l, k in order:
        if (l, k) != (0, 0):
            loads[l, k].start()
        owns[l, k].start()

    load_q.wait()
    q32 = qraw[...].astype(f32)
    for h in range(KVH):
        rows = [q32[l:l + 1, (h * GROUP + g) * HD:(h * GROUP + g + 1) * HD]
                for l in range(2) for g in range(GROUP)]
        qmsg[h] = jnp.concatenate(rows, axis=0).astype(bf16)
    loads[0, 0].wait()
    pl.semaphore_wait(barrier, len(peers))

    for k in range(1, 8):
        to = (head + k) % 8
        remote(qmsg.at[to], qa.at[head], a_sem.at[0], a_sem.at[1], at(to, yl, z, c)).start()
    qa[head] = qmsg[head]

    def kv_send(l, k, steps):
        for dz, dy in steps:
            yl_to, zl_to = (yl + dy) % 2, (zl + dz) % 4
            to = yl_to * 4 + zl_to
            remote(
                stage.at[l, k, :, pl.ds(pl.multiple_of(to * POS, POS), POS)],
                kown.at[l, k, part], kv_s.at[l * 2 + k],
                v1_r.at[part] if (l, k) == (1, 1) else kv_r.at[l * 2 + k],
                at(head, yl_to, zh * 4 + zl_to, c)).start()

    def kv_wait(l, k):
        owns[l, k].wait()
        remote(kown.at[l, k, 0:7], kown.at[l, k, 0:7], kv_s.at[0], kv_r.at[l * 2 + k]).wait_recv()

    def forward(l, k):
        return remote(kown.at[l, k], koth.at[l, k], f_s.at[l * 2 + k], f_r.at[l * 2 + k])

    early = [(2, 0), (2, 1), (0, 1), (1, 0)]
    late = [(1, 1), (3, 0), (3, 1)]
    full = [(2, 0), (2, 1), (1, 0), (1, 1), (3, 0), (3, 1), (0, 1)]

    kv_send(0, 0, early)

    load_suf.wait()
    count = lengths[slot[0]]
    row = lax.broadcasted_iota(jnp.int32, (8, HD), 0)
    lane = lax.broadcasted_iota(jnp.int32, (8, HD), 1)
    valid = lane < count

    def suffix_head(h):
        cols = slice(h * HD, (h + 1) * HD)
        q = qmsg[h]
        s0 = dot(q, suf[0, 0, 0, :, cols], NT)
        s1 = dot(q, suf[1, 0, 0, :, cols], NT)
        s = jnp.where(valid, jnp.where(row < GROUP, s0, s1) * SCALE2, NEG)
        top = jnp.max(s, axis=1, keepdims=True)
        w = jnp.where(valid, jnp.exp2(s - top), 0.0).astype(bf16)
        den = jnp.sum(w.astype(f32), axis=1, keepdims=True)
        n0 = dot(w, suf[0, 0, 1, :, cols], NN)
        n1 = dot(w, suf[1, 0, 1, :, cols], NN)
        sbuf_o[h] = jnp.where(row < GROUP, n0, n1) / den
        sbuf_l[h] = jnp.broadcast_to(top + jnp.log2(den), (8, HD))

    def suffix_part():
        for h in range(KVH):
            suffix_head(h)

    suffix_part()

    def a_wait():
        remote(qa.at[0:7], qa.at[0:7], a_sem.at[0], a_sem.at[1]).wait_recv()

    a_wait()
    qall[z, yl] = jnp.swapaxes(qa[...].astype(f32), 0, 1).reshape(64, HD).astype(bf16)
    loads[1, 0].wait()
    for k in (4, 3, 5, 2, 6, 1, 7):
        remote(qall.at[z, yl], qall.at[z, yl], b_sem.at[0], b_sem.at[1],
               at(head, yl, (z + k) % 8, c)).start()
    kv_send(0, 0, late)
    kv_send(1, 0, full)
    loads[0, 1].wait()
    loads[1, 1].wait()

    def b_wait():
        remote(qall.at[0:7, 0], qall.at[0:7, 0], b_sem.at[0], b_sem.at[1]).wait_recv()

    def y_copy(which):
        return remote(qall.at[:, which], qall.at[:, which], y_sem.at[0], y_sem.at[1],
                      at(head, 1 - yl, z, c))

    def y_wait():
        y_copy(1 - yl).wait_recv()

    b_wait()
    y_copy(yl).start()
    kv_send(0, 1, full)
    kv_send(1, 1, full)

    def weights(l):
        forward(l, 0).wait_recv()
        r64 = lax.broadcasted_iota(jnp.int32, (2, 64, HD), 1)
        c64 = lax.broadcasted_iota(jnp.int32, (2, 64, HD), 2)

        def rows(i, carry):
            q = qall[pl.ds(i * 2, 2), :, l * 32:(l + 1) * 32, :].reshape(128, HD)
            at_rows = pl.ds(pl.multiple_of(i * 128, 128), 128)
            sa = dot(q, kown[l, 0].reshape(HD, POS), NN) * SCALE2
            sb = dot(q, koth[l, 0].reshape(HD, POS), NN) * SCALE2
            top = jnp.maximum(jnp.max(sa, axis=1, keepdims=True), jnp.max(sb, axis=1, keepdims=True))
            wa = jnp.exp2(sa - top).astype(bf16)
            wb = jnp.exp2(sb - top).astype(bf16)
            den = jnp.sum(wa.astype(f32) + wb.astype(f32), axis=1, keepdims=True)
            wbuf[l, 0, at_rows, :] = wa
            wbuf[l, 1, at_rows, :] = wb
            rden[l, at_rows, :] = jnp.broadcast_to(1.0 / den, (128, HD))
            big = jnp.broadcast_to(top + jnp.log2(den), (128, HD)).reshape(2, 64, HD)
            line = jnp.sum(jnp.where(c64 == r64 + l * 64, big, 0.0), axis=1, keepdims=True)
            if l == 0:
                lsend[pl.ds(i * 2, 2)] = line
            else:
                lsend[pl.ds(i * 2, 2)] = lsend[pl.ds(i * 2, 2)] + line
            return carry

        lax.fori_loop(0, 4, rows, 0)

    def values_own(l):
        def rows(i, carry):
            at_rows = pl.ds(pl.multiple_of(i * 128, 128), 128)
            oacc[at_rows, :] = dot(wbuf[l, 0, at_rows, :], kown[l, 1].reshape(HD, POS), NT)
            return carry

        lax.fori_loop(0, 4, rows, 0)

    def values_other(l):
        forward(l, 1).wait_recv()
        for i in range(4):
            at_rows = slice(i * 128, (i + 1) * 128)
            o = oacc[at_rows, :] + dot(wbuf[l, 1, at_rows, :], koth[l, 1].reshape(HD, POS), NT)
            o = o * rden[l, at_rows, :]
            osend[l, 2 * i:2 * i + 2] = o.astype(bf16).reshape(2, 64, HD)
            for to in (2 * i, 2 * i + 1):
                @pl.when(z != to)
                def _():
                    remote(osend.at[l, to], orecv.at[l, z], c_s.at[l], c_r.at[l],
                           at(head, yl, to, c)).start()
        orecv[l, z] = osend[l, z]

    kv_wait(0, 0)
    forward(0, 0).start()
    y_wait()
    weights(0)
    kv_wait(1, 0)
    forward(1, 0).start()
    weights(1)
    for k in range(1, 8):
        to = (z + k) % 8
        remote(lsend.at[to], lrecv.at[z], l_sem.at[0], l_sem.at[1], at(head, yl, to, c)).start()
    lrecv[z] = lsend[z]
    kv_wait(0, 1)
    forward(0, 1).start()
    values_own(0)
    values_other(0)

    def last_pieces():
        owns[1, 1].wait()
        remote(kown.at[1, 1, part], koth.at[1, 1, part], f_s.at[3], f_r.at[3]).start()
        for dz, dy in full:
            src = (yl + dy) % 2 * 4 + (zl + 4 - dz) % 4
            piece = kown.at[1, 1, src]
            remote(piece, piece, kv_s.at[0], v1_r.at[src]).wait_recv()
            remote(piece, koth.at[1, 1, src], f_s.at[3], f_r.at[3]).start()

    last_pieces()
    values_own(1)
    values_other(1)

    def sources():
        remote(lrecv.at[0:7], lrecv.at[0:7], l_sem.at[0], l_sem.at[1]).wait_recv()
        ls = lrecv[...].reshape(8, HD)
        top = jnp.max(ls, axis=0, keepdims=True)
        w = jnp.exp2(ls - top)
        den = jnp.sum(w, axis=0, keepdims=True)
        total = jnp.broadcast_to(top + jnp.log2(den), (120, HD))
        cols = jnp.concatenate([w / den, total], axis=0).T
        big = jnp.broadcast_to(cols[:, 8:9], (128, HD)).reshape(2, 2, GROUP, 8, HD)
        both = [jnp.swapaxes(big[:, to].reshape(8, 8, HD), 0, 1) for to in range(2)]
        gsend[...] = jnp.stack(both, axis=1).reshape(16, 8, HD)
        for k in range(1, 16):
            to = (spot + k) % 16
            remote(gsend.at[to], grecv.at[spot], g_sem.at[0], g_sem.at[1],
                   at(to // 2, to % 2, z, c)).start()
        grecv[spot] = gsend[spot]
        return cols

    def combine(l, cols):
        remote(orecv.at[l, 0:7], orecv.at[l, 0:7], c_s.at[l], c_r.at[l]).wait_recv()
        o = jnp.zeros((64, HD), f32)
        for s in range(8):
            o = o + orecv[l, s].astype(f32) * cols[l * 64:(l + 1) * 64, s:s + 1]
        o = o.reshape(2, GROUP, 8, HD)
        both = [jnp.swapaxes(o[to], 0, 1) for to in range(2)]
        fsend[l] = jnp.stack(both, axis=1).reshape(16, GROUP, HD)
        for k in range(1, 16):
            to = (spot + k) % 16
            remote(fsend.at[l, to], frecv.at[l, spot], d_s.at[l], d_r.at[l],
                   at(to // 2, to % 2, z, c)).start()
        frecv[l, spot] = fsend[l, spot]

    cols = sources()
    combine(0, cols)
    combine(1, cols)

    def shares():
        remote(grecv.at[0:15], grecv.at[0:15], g_sem.at[0], g_sem.at[1]).wait_recv()
        g = grecv[...].reshape(KVH, 2, 8, HD)
        la, lb, lc = g[:, 0], g[:, 1], sbuf_l[...]
        top = jnp.maximum(jnp.maximum(la, lb), lc)
        a, b, s = jnp.exp2(la - top), jnp.exp2(lb - top), jnp.exp2(lc - top)
        den = a + b + s
        return a / den, b / den, s / den * sbuf_o[...]

    def finish(l, a, b, s):
        remote(frecv.at[l, 0:15], frecv.at[l, 0:15], d_s.at[l], d_r.at[l]).wait_recv()
        part_of = slice(l * GROUP, (l + 1) * GROUP)
        got = frecv[l].reshape(KVH, 2, GROUP, HD)
        return got[:, 0] * a[:, part_of] + got[:, 1] * b[:, part_of] + s[:, part_of]

    a, b, s = shares()
    o0 = finish(0, a, b, s)
    o1 = finish(1, a, b, s)
    for h in range(KVH):
        for g in range(GROUP):
            pair = jnp.concatenate([o0[h, g:g + 1], o1[h, g:g + 1]], axis=0)
            out[:, (h * GROUP + g) * HD:(h * GROUP + g + 1) * HD] = pair.astype(bf16)

    remote(qa.at[0:7], qa.at[0:7], a_sem.at[0], a_sem.at[1]).wait_send()
    remote(qall.at[0:7, 0], qall.at[0:7, 0], b_sem.at[0], b_sem.at[1]).wait_send()
    y_copy(yl).wait_send()
    remote(lrecv.at[0:7], lrecv.at[0:7], l_sem.at[0], l_sem.at[1]).wait_send()
    remote(grecv.at[0:15], grecv.at[0:15], g_sem.at[0], g_sem.at[1]).wait_send()
    for l in range(2):
        for k in range(2):
            remote(kown.at[l, k, 0:7], kown.at[l, k, 0:7], kv_s.at[l * 2 + k], kv_r.at[0]).wait_send()
            forward(l, k).wait_send()
        remote(orecv.at[l, 0:7], orecv.at[l, 0:7], c_s.at[l], c_r.at[l]).wait_send()
        remote(frecv.at[l, 0:15], frecv.at[l, 0:15], d_s.at[l], d_r.at[l]).wait_send()


def body(prefix_cache, queries, suffix_cache, suffix_lengths, slot_request):
    bf, f32 = jnp.bfloat16, jnp.float32
    dma = pltpu.SemaphoreType.DMA
    any_space = pl.BlockSpec(memory_space=pl.ANY)
    out = pl.pallas_call(
        kernel,
        out_shape=jax.ShapeDtypeStruct((2, QH * HD), bf),
        in_specs=[
            any_space,
            any_space,
            any_space,
            pl.BlockSpec(memory_space=pltpu.SMEM),
            pl.BlockSpec(memory_space=pltpu.SMEM),
        ],
        out_specs=pl.BlockSpec(memory_space=pltpu.VMEM),
        scratch_shapes=[
            pltpu.VMEM((2, 2, 16, 8192), bf),
            pltpu.VMEM((2, 2, 8, 16, POS), bf),
            pltpu.VMEM((2, 2, 8, 16, POS), bf),
            pltpu.VMEM((2, 1, 2, SUF, KVH * HD), bf),
            pltpu.VMEM((2, QH * HD), bf),
            pltpu.VMEM((8, 8, HD), bf),
            pltpu.VMEM((8, 8, HD), bf),
            pltpu.VMEM((8, 2, 64, HD), bf),
            pltpu.VMEM((2, 2, 512, POS), bf),
            pltpu.VMEM((2, 512, HD), f32),
            pltpu.VMEM((512, HD), f32),
            pltpu.VMEM((KVH, 8, HD), f32),
            pltpu.VMEM((KVH, 8, HD), f32),
            pltpu.VMEM((2, 8, 64, HD), bf),
            pltpu.VMEM((2, 8, 64, HD), bf),
            pltpu.VMEM((8, 1, HD), f32),
            pltpu.VMEM((8, 1, HD), f32),
            pltpu.VMEM((16, 8, HD), f32),
            pltpu.VMEM((16, 8, HD), f32),
            pltpu.VMEM((2, 16, GROUP, HD), f32),
            pltpu.VMEM((2, 16, GROUP, HD), f32),
            dma((10,)),
            dma((2,)), dma((2,)), dma((2,)),
            dma((4,)), dma((4,)), dma((8,)),
            dma((4,)), dma((4,)),
            dma((2,)), dma((2,)),
            dma((2,)), dma((2,)),
            dma((2,)), dma((2,)),
        ],
        compiler_params=pltpu.CompilerParams(collective_id=0, has_side_effects=True),
        name="attend",
    )(prefix_cache, queries.reshape(2, QH * HD), suffix_cache, suffix_lengths, slot_request)
    return out.reshape(2, 1, QH * HD)


def solution(mesh):
    in_specs = (
        P(None, None, "seq", "rep"),
        P(None, ("seq", "rep"), None),
        P(None, ("seq", "rep"), None, None, None),
        P(),
        P(("seq", "rep")),
    )
    out_specs = P(None, ("seq", "rep"), None)
    return jax.shard_map(body, mesh=mesh, in_specs=in_specs, out_specs=out_specs, check_vma=False)
```

time: 60.2 us -> 54.3 us (0.902)
  Pallas kernels: 56.5 us -> 51.4 us
  local copies, waits for them, and re-layouts: 2.69 us -> 1.34 us
    pallas_call x1, Pallas kernels: 56.5 us -> 51.4 us  [body(): pl.pallas_call(kernel, out_shape=jax.ShapeDtypeStruct((2, QH * HD), bf),...]
    reshape x3 -> x0, local copies, waits for them, and re-layouts: 2.69 us -> none  [the longest x2 1.35 us: body(): queries.reshape(2, KVH, GROUP, HD).transpose(1, 0, 2, 3)]
    unnamed x0 -> x1, local copies, waits for them, and re-layouts: none -> 1.34 us
where the time goes in v2:
time: 54.3 us; the launch traced here: 53.4 us
  Pallas kernels  51.4 us (95%)
  local copies, waits for them, and re-layouts  1.34 us (2%)
  between operations  0.66 us (1%)
    pallas_call x1, Pallas kernels, body(): pl.pallas_call(kernel, out_shape=jax.ShapeDtypeStruct((2, QH * HD), bf),...  51.4 us
    unnamed x1, local copies, waits for them, and re-layouts  1.34 us

profile of v2, /device:TPU:1, one launch (start us, length us, event | category | flops | bytes accessed | tf_op | source)
XLA Modules:
  0.0 53.4 jit_solution(11844676696189494504)
XLA Ops:
  0.7 51.4 %attend.1 = bf16[2,4096]{1,0:T(2,128)(2,1)} custom-call(bf16[2,2,16,8192]{3,2,1,0:T(8,128)(2,1)} %prefix.1, bf16[2,4096]{1,0:T(2,128)(2,1)} %bitcast.3, bf16[2,1,2,128,1024]{4,3,2,1,0:T(8,128)(2,1)} %suffix.1, s32[256]{0:T(256)} %lengths.1, s32[1]{0:T(128)S(6)} %copy.7.slot), custom_call_target="tpu_custom_call" | custom-call | tf_op jit(solution)/shard_map/attend/pallas_call | solution.py:328
  52.1 1.3 %copy.8 = bf16[2,1,4096]{2,0,1:T(2,128)(2,1)} copy(bf16[2,1,4096]{2,0,1:T(2,128)(2,1)} %bitcast.2) | data formatting | bytes 32768

commit v3 on v2

v3 whole, which is shorter than its diff:
```python
import math

import jax
import jax.numpy as jnp
from jax import lax
from jax.experimental import pallas as pl
from jax.experimental.pallas import tpu as pltpu
from jax.sharding import PartitionSpec as P

QH = 32
KVH = 8
HD = 128
SUF = 128
GROUP = 4
NEG = -1e30
SCALE2 = HD ** -0.5 * math.log2(math.e)
POS = 1024
HALF = POS // 2
NT = (((1,), (1,)), ((), ()))
NN = (((1,), (0,)), ((), ()))
MESH = pl.DeviceIdType.MESH


def dot(a, b, dims):
    return lax.dot_general(a, b, dims, preferred_element_type=jnp.float32)


def kernel(
    prefix, queries, suffix, lengths_in, slot_in, out,
    lengths, slot, stage, kown, koth, suf, qraw, qmsg, qa, qall, wbuf, rden, oacc, sbuf_o, sbuf_l,
    osend, orecv, lsend, lrecv, gsend, grecv, share,
    loc_sem, a_sem, b_sem, y_sem, kv_s, kv_r, v1_r, f_s, f_r, c_s, c_r, l_sem, g_sem,
):
    f32, bf16 = jnp.float32, jnp.bfloat16
    seq = lax.axis_index("seq")
    rep = lax.axis_index("rep")
    x, y, zl = seq // 16, (seq // 4) % 4, seq % 4
    yh, yl = y // 2, y % 2
    zh, c = rep // 2, rep % 2
    z = zh * 4 + zl
    head = x * 2 + yh
    part = yl * 4 + zl
    spot = head * 2 + yl

    def at(head_to, yl_to, z_to, c_to):
        x_to, yh_to = head_to // 2, head_to % 2
        return ((x_to * 4 + yh_to * 2 + yl_to) * 4 + z_to % 4, (z_to // 4) * 2 + c_to)

    other = at(head, yl, z, 1 - c)

    def remote(src, dst, s, r, dev=other):
        return pltpu.make_async_remote_copy(
            src_ref=src, dst_ref=dst, send_sem=s, recv_sem=r, device_id=dev, device_id_type=MESH)

    load_q = pltpu.make_async_copy(queries, qraw, loc_sem.at[9])
    load_q.start()
    barrier = pltpu.get_barrier_semaphore()
    peers = [other]
    for k in range(1, 16):
        to = (spot + k) % 16
        peers.append(at(to // 2, to % 2, z, c))
    for k in range(1, 8):
        peers.append(at(head, yl, (z + k) % 8, c))
    for k in range(1, 4):
        peers.append(at(head, 1 - yl, zh * 4 + (zl + k) % 4, c))
    for dev in peers:
        pl.semaphore_signal(barrier, inc=1, device_id=dev, device_id_type=MESH)

    order = ((0, 0), (1, 0), (0, 1), (1, 1))
    loads = {(l, k): pltpu.make_async_copy(prefix.at[l, k], stage.at[l, k], loc_sem.at[l * 2 + k])
             for l, k in order}
    owns = {(l, k): pltpu.make_async_copy(
        prefix.at[l, k, :, pl.ds(pl.multiple_of(part * POS, POS), POS)],
        kown.at[l, k, part], loc_sem.at[4 + l * 2 + k]) for l, k in order}
    load_suf = pltpu.make_async_copy(suffix, suf, loc_sem.at[8])
    load_len = pltpu.make_async_copy(lengths_in, lengths, loc_sem.at[10])
    load_slot = pltpu.make_async_copy(slot_in, slot, loc_sem.at[11])
    loads[0, 0].start()
    load_suf.start()
    load_len.start()
    load_slot.start()

    for l, k in order:
        if (l, k) != (0, 0):
            loads[l, k].start()
        owns[l, k].start()

    load_q.wait()
    q32 = qraw[...].astype(f32)
    for h in range(KVH):
        rows = [q32[l:l + 1, (h * GROUP + g) * HD:(h * GROUP + g + 1) * HD]
                for l in range(2) for g in range(GROUP)]
        qmsg[h] = jnp.concatenate(rows, axis=0).astype(bf16)
    loads[0, 0].wait()
    pl.semaphore_wait(barrier, len(peers))

    for k in range(1, 8):
        to = (head + k) % 8
        remote(qmsg.at[to], qa.at[head], a_sem.at[0], a_sem.at[1], at(to, yl, z, c)).start()
    qa[head] = qmsg[head]

    def kv_send(l, k, steps, half=None):
        for dz, dy in steps:
            yl_to, zl_to = (yl + dy) % 2, (zl + dz) % 4
            to = yl_to * 4 + zl_to
            if half is None:
                start, size, dst, r = 0, POS, kown.at[l, k, part], kv_r.at[l * 2 + k]
            else:
                start, size = half * HALF, HALF
                dst = kown.at[l, k, part, :, start:start + HALF]
                r = v1_r.at[part] if half else kv_r.at[l * 2 + k]
            remote(
                stage.at[l, k, :, pl.ds(pl.multiple_of(to * POS + start, HALF), size)],
                dst, kv_s.at[l * 2 + k], r, at(head, yl_to, zh * 4 + zl_to, c)).start()

    def kv_wait(l, k):
        owns[l, k].wait()
        remote(kown.at[l, k, 0:7], kown.at[l, k, 0:7], kv_s.at[0], kv_r.at[l * 2 + k]).wait_recv()

    def forward(l, k):
        return remote(kown.at[l, k], koth.at[l, k], f_s.at[l * 2 + k], f_r.at[l * 2 + k])

    full = [(2, 0), (2, 1), (1, 0), (1, 1), (3, 0), (3, 1), (0, 1)]

    kv_send(0, 0, [(2, 0), (2, 1), (0, 1), (1, 0)])

    load_suf.wait()
    load_len.wait()
    load_slot.wait()
    count = lengths[slot[0]]
    row = lax.broadcasted_iota(jnp.int32, (8, HD), 0)
    lane = lax.broadcasted_iota(jnp.int32, (8, HD), 1)
    valid = lane < count

    def suffix_head(h):
        cols = slice(h * HD, (h + 1) * HD)
        q = qmsg[h]
        s0 = dot(q, suf[0, 0, 0, :, cols], NT)
        s1 = dot(q, suf[1, 0, 0, :, cols], NT)
        s = jnp.where(valid, jnp.where(row < GROUP, s0, s1) * SCALE2, NEG)
        top = jnp.max(s, axis=1, keepdims=True)
        w = jnp.where(valid, jnp.exp2(s - top), 0.0).astype(bf16)
        den = jnp.sum(w.astype(f32), axis=1, keepdims=True)
        n0 = dot(w, suf[0, 0, 1, :, cols], NN)
        n1 = dot(w, suf[1, 0, 1, :, cols], NN)
        sbuf_o[h] = jnp.where(row < GROUP, n0, n1) / den
        sbuf_l[h] = jnp.broadcast_to(top + jnp.log2(den), (8, HD))

    def suffix_part():
        for h in range(KVH):
            suffix_head(h)

    suffix_part()

    def a_wait():
        remote(qa.at[0:7], qa.at[0:7], a_sem.at[0], a_sem.at[1]).wait_recv()

    a_wait()
    low = row < GROUP

    def regroup(a, b):
        return (jnp.where(low, a, pltpu.roll(b, GROUP, 0)), jnp.where(low, pltpu.roll(a, GROUP, 0), b))

    pairs = [regroup(qa[2 * j].astype(f32), qa[2 * j + 1].astype(f32)) for j in range(4)]
    qall[z, yl] = jnp.concatenate([p[l] for l in range(2) for p in pairs], axis=0).astype(bf16)
    line = (z + 2) % 8

    def mate(k):
        return (line // 4 * 4 + (line + k) % 4 + 6) % 8

    mirror = zh * 4 + 3 - zl

    def b_send(block, z_to, r):
        remote(qall.at[block, yl], qall.at[block, yl], b_sem.at[0], r, at(head, yl, z_to, c)).start()

    b_send(z, mirror, b_sem.at[2])
    for k in (2, 1, 3):
        b_send(z, mate(k), b_sem.at[1])
    loads[1, 0].wait()
    kv_send(0, 0, [(1, 1), (3, 0), (3, 1)])
    kv_send(1, 0, [(2, 0)])

    def m_wait():
        remote(qall.at[mirror, yl], qall.at[mirror, yl], b_sem.at[0], b_sem.at[2]).wait_recv()

    m_wait()
    for k in (2, 1, 3):
        b_send(mirror, mate(k), b_sem.at[1])
    loads[0, 1].wait()
    kv_send(1, 0, full[1:])
    kv_send(0, 1, full[:2])
    kv_wait(0, 0)
    forward(0, 0).start()

    def b_wait():
        remote(qall.at[0:6, 0], qall.at[0:6, 0], b_sem.at[0], b_sem.at[1]).wait_recv()

    def y_copy(which):
        return remote(qall.at[:, which], qall.at[:, which], y_sem.at[0], y_sem.at[1],
                      at(head, 1 - yl, z, c))

    def y_wait():
        y_copy(1 - yl).wait_recv()

    b_wait()
    y_copy(yl).start()
    kv_send(0, 1, full[2:])
    loads[1, 1].wait()

    def weights(l):
        forward(l, 0).wait_recv()
        r64 = lax.broadcasted_iota(jnp.int32, (2, 64, HD), 1)
        c64 = lax.broadcasted_iota(jnp.int32, (2, 64, HD), 2)

        def rows(i, carry):
            q = qall[pl.ds(i * 2, 2), :, l * 32:(l + 1) * 32, :].reshape(128, HD)
            at_rows = pl.ds(pl.multiple_of(i * 128, 128), 128)
            sa = dot(q, kown[l, 0].reshape(HD, POS), NN) * SCALE2
            sb = dot(q, koth[l, 0].reshape(HD, POS), NN) * SCALE2
            top = jnp.maximum(jnp.max(sa, axis=1, keepdims=True), jnp.max(sb, axis=1, keepdims=True))
            wa = jnp.exp2(sa - top).astype(bf16)
            wb = jnp.exp2(sb - top).astype(bf16)
            den = jnp.sum(wa.astype(f32) + wb.astype(f32), axis=1, keepdims=True)
            wbuf[l, 0, at_rows, :] = wa
            wbuf[l, 1, at_rows, :] = wb
            rden[l, at_rows, :] = jnp.broadcast_to(1.0 / den, (128, HD))
            big = jnp.broadcast_to(top + jnp.log2(den), (128, HD)).reshape(2, 64, HD)
            line = jnp.sum(jnp.where(c64 == r64 + l * 64, big, 0.0), axis=1, keepdims=True)
            if l == 0:
                lsend[pl.ds(i * 2, 2)] = line
            else:
                lsend[pl.ds(i * 2, 2)] = lsend[pl.ds(i * 2, 2)] + line
            return carry

        lax.fori_loop(0, 4, rows, 0, unroll=True)

    def partials(l):
        def ring(j, carry):
            dz = 4 + (j + 1) // 2 * (1 - 2 * (j % 2))
            z_to = (z + dz) % 8
            for i in range(15, -1, -1):
                spot_to = (spot + i) % 16
                copy = remote(
                    osend.at[l, z_to * 16 + spot_to % 2 * 8 + spot_to // 2], orecv.at[l, spot * 8 + z],
                    c_s.at[l], c_r.at[l], at(spot_to // 2, spot_to % 2, z_to, c))
                if i:
                    copy.start()
                else:
                    pl.when(dz != 0)(copy.start)
            return carry

        lax.fori_loop(0, 8, ring, 0)
        orecv[l, spot * 8 + z] = osend[l, z * 16 + yl * 8 + head]

    def store_partials(l, o):
        osend.at[l].reshape(512, HD)[...] = o.astype(bf16)

    def values_own(l):
        oacc[l] = dot(wbuf[l, 0], kown[l, 1].reshape(HD, POS), NT)

    def values_other(l):
        forward(l, 1).wait_recv()
        store_partials(l, (oacc[l] + dot(wbuf[l, 1], koth[l, 1].reshape(HD, POS), NT)) * rden[l])

    def sources():
        remote(lrecv.at[0:7], lrecv.at[0:7], l_sem.at[0], l_sem.at[1]).wait_recv()
        ls = jnp.concatenate([lrecv[...].reshape(8, HD), jnp.full((120, HD), NEG, f32)], axis=0).T
        for half in range(2):
            for j in range(4):
                base = half * 32 + j * 8
                even, odd = regroup(ls[base:base + 8], ls[64 + base:72 + base])
                gsend[4 * j + half] = even
                gsend[4 * j + 2 + half] = odd
        for k in range(1, 16):
            to = (spot + k) % 16
            remote(gsend.at[to], grecv.at[spot], g_sem.at[0], g_sem.at[1],
                   at(to // 2, to % 2, z, c)).start()
        grecv[spot] = gsend[spot]

    kv_wait(1, 0)
    forward(1, 0).start()
    kv_send(1, 1, full, 0)
    y_wait()
    weights(0)
    kv_send(1, 1, full, 1)
    weights(1)
    for k in range(1, 8):
        to = (z + k) % 8
        remote(lsend.at[to], lrecv.at[z], l_sem.at[0], l_sem.at[1], at(head, yl, to, c)).start()
    lrecv[z] = lsend[z]
    kv_wait(0, 1)
    forward(0, 1).start()
    values_own(0)

    first, second = slice(0, HALF), slice(HALF, POS)

    def last_first():
        owns[1, 1].wait()
        piece = kown.at[1, 1, 0:7, :, first]
        remote(piece, piece, kv_s.at[0], kv_r.at[3]).wait_recv()

    def last_copy():
        return remote(kown.at[1, 1, :, :, first], koth.at[1, 1, :, :, first], f_s.at[4], f_r.at[4])

    def last_dot(which, ref, span):
        return dot(wbuf[1, which, :, span], ref[1, 1, :, :, span].reshape(HD, HALF), NT)

    def values_first():
        oacc[1] = last_dot(0, kown, first)

    def last_pieces():
        own = kown.at[1, 1, part, :, second]
        remote(own, koth.at[1, 1, part, :, second], f_s.at[3], f_r.at[3]).start()
        for dz, dy in full:
            src = (yl + dy) % 2 * 4 + (zl + 4 - dz) % 4
            piece = kown.at[1, 1, src, :, second]
            remote(piece, piece, kv_s.at[0], v1_r.at[src]).wait_recv()
            remote(piece, koth.at[1, 1, src, :, second], f_s.at[3], f_r.at[3]).start()

    def values_second():
        oacc[1] = oacc[1] + last_dot(0, kown, second)
        last_copy().wait_recv()
        oacc[1] = oacc[1] + last_dot(1, koth, first)
        whole = koth.at[1, 1, :, :, second]
        remote(whole, whole, f_s.at[3], f_r.at[3]).wait_recv()
        store_partials(1, (oacc[1] + last_dot(1, koth, second)) * rden[1])

    last_first()
    last_copy().start()
    values_first()
    values_other(0)
    partials(0)
    last_pieces()
    sources()
    values_second()
    partials(1)

    def shares():
        remote(grecv.at[0:15], grecv.at[0:15], g_sem.at[0], g_sem.at[1]).wait_recv()

        def one_head(h, carry):
            la, lb, lc = grecv[2 * h], grecv[2 * h + 1], sbuf_l[h]
            top = jnp.max(jnp.maximum(jnp.maximum(la, lb), lc), axis=1, keepdims=True)
            a, b, s = jnp.exp2(la - top), jnp.exp2(lb - top), jnp.exp2(lc - top)
            den = jnp.sum(a + b, axis=1, keepdims=True) + s
            sbuf_o[h] = s / den * sbuf_o[h]
            for half, w in enumerate((a / den, b / den)):
                for j in range(4):
                    pair = [jnp.broadcast_to(w[:, k:k + 1], (8, HD)) for k in (2 * j, 2 * j + 1)]
                    for l, tile in enumerate(regroup(*pair)):
                        share[l, 2 * h + half, j] = tile
            return carry

        lax.fori_loop(0, KVH, one_head, 0)

    def finish(l):
        remote(orecv.at[l, 0:127], orecv.at[l, 0:127], c_s.at[l], c_r.at[l]).wait_recv()
        got = orecv.at[l].reshape(512, HD)[...].astype(f32).reshape(KVH, 8, 8, HD)
        return jnp.sum(got * share[l].reshape(KVH, 8, 8, HD), axis=1)

    shares()
    o0 = finish(0)
    o1 = finish(1)
    for h in range(KVH):
        first_half, last_half = regroup(o0[h], o1[h])
        both = first_half + last_half + sbuf_o[h]
        for g in range(GROUP):
            pair = jnp.concatenate([both[g:g + 1], both[GROUP + g:GROUP + g + 1]], axis=0)
            out[:, (h * GROUP + g) * HD:(h * GROUP + g + 1) * HD] = pair.astype(bf16)

    remote(qa.at[0:7], qa.at[0:7], a_sem.at[0], a_sem.at[1]).wait_send()
    remote(qall.at[0:7, 0], qall.at[0:7, 0], b_sem.at[0], b_sem.at[1]).wait_send()
    y_copy(yl).wait_send()
    last_copy().wait_send()
    remote(kown.at[1, 1, :, :, second], koth.at[1, 1, :, :, second], f_s.at[3], f_r.at[3]).wait_send()
    remote(lrecv.at[0:7], lrecv.at[0:7], l_sem.at[0], l_sem.at[1]).wait_send()
    remote(grecv.at[0:15], grecv.at[0:15], g_sem.at[0], g_sem.at[1]).wait_send()
    for l in range(2):
        for k in range(2):
            remote(kown.at[l, k, 0:7], kown.at[l, k, 0:7], kv_s.at[l * 2 + k], kv_r.at[0]).wait_send()
            if (l, k) != (1, 1):
                forward(l, k).wait_send()
        remote(orecv.at[l, 0:127], orecv.at[l, 0:127], c_s.at[l], c_r.at[l]).wait_send()


def body(prefix_cache, queries, suffix_cache, suffix_lengths, slot_request):
    bf, f32 = jnp.bfloat16, jnp.float32
    dma = pltpu.SemaphoreType.DMA
    any_space = pl.BlockSpec(memory_space=pl.ANY)
    out = pl.pallas_call(
        kernel,
        out_shape=pltpu.VMEM((2, QH * HD), bf),
        in_specs=[
            any_space,
            any_space,
            any_space,
            any_space,
            any_space,
        ],
        out_specs=pl.BlockSpec(memory_space=pltpu.VMEM),
        scratch_shapes=[
            pltpu.SMEM((256,), jnp.int32),
            pltpu.SMEM((1,), jnp.int32),
            pltpu.VMEM((2, 2, 16, 8192), bf),
            pltpu.VMEM((2, 2, 8, 16, POS), bf),
            pltpu.VMEM((2, 2, 8, 16, POS), bf),
            pltpu.VMEM((2, 1, 2, SUF, KVH * HD), bf),
            pltpu.VMEM((2, QH * HD), bf),
            pltpu.VMEM((8, 8, HD), bf),
            pltpu.VMEM((8, 8, HD), bf),
            pltpu.VMEM((8, 2, 64, HD), bf),
            pltpu.VMEM((2, 2, 512, POS), bf),
            pltpu.VMEM((2, 512, HD), f32),
            pltpu.VMEM((2, 512, HD), f32),
            pltpu.VMEM((KVH, 8, HD), f32),
            pltpu.VMEM((KVH, 8, HD), f32),
            pltpu.VMEM((2, 128, GROUP, HD), bf),
            pltpu.VMEM((2, 128, GROUP, HD), bf),
            pltpu.VMEM((8, 1, HD), f32),
            pltpu.VMEM((8, 1, HD), f32),
            pltpu.VMEM((16, 8, HD), f32),
            pltpu.VMEM((16, 8, HD), f32),
            pltpu.VMEM((2, 16, 4, 8, HD), f32),
            dma((12,)),
            dma((2,)), dma((3,)), dma((2,)),
            dma((4,)), dma((4,)), dma((8,)),
            dma((5,)), dma((5,)),
            dma((2,)), dma((2,)),
            dma((2,)), dma((2,)),
        ],
        compiler_params=pltpu.CompilerParams(collective_id=0, has_side_effects=True),
        name="attend",
    )(prefix_cache, queries.reshape(2, QH * HD), suffix_cache, suffix_lengths, slot_request)
    return out.reshape(2, 1, QH * HD)


def solution(mesh):
    in_specs = (
        P(None, None, "seq", "rep"),
        P(None, ("seq", "rep"), None),
        P(None, ("seq", "rep"), None, None, None),
        P(),
        P(("seq", "rep")),
    )
    out_specs = P(None, ("seq", "rep"), None)
    return jax.shard_map(body, mesh=mesh, in_specs=in_specs, out_specs=out_specs, check_vma=False)
```

time: 54.3 us -> 48.9 us (0.901); the launches traced: 53.4 us -> 48.7 us
  Pallas kernels: 51.4 us -> 47.4 us
  local copies, waits for them, and re-layouts: 1.34 us -> 0.61 us
    pallas_call x1, Pallas kernels: 51.4 us -> 47.4 us  [body(): pl.pallas_call(kernel, out_shape=pltpu.VMEM((2, QH * HD), bf), in_specs=[...]
    unnamed x1, local copies, waits for them, and re-layouts: 1.34 us -> 0.61 us
where the time goes in v3:
time: 48.9 us; the launch traced here: 48.7 us
  Pallas kernels  47.4 us (97%)
  between operations  0.66 us (1%)
  local copies, waits for them, and re-layouts  0.61 us (1%)
    pallas_call x1, Pallas kernels, body(): pl.pallas_call(kernel, out_shape=pltpu.VMEM((2, QH * HD), bf), in_specs=[...  47.4 us

profile of v3, /device:TPU:1, one launch (start us, length us, event | category | flops | bytes accessed | tf_op | source)
XLA Modules:
  0.0 48.7 jit_solution(3860809598373206438)
XLA Ops:
  0.7 47.4 %attend.1 = bf16[2,4096]{1,0:T(2,128)(2,1)S(1)} custom-call(bf16[2,2,16,8192]{3,2,1,0:T(8,128)(2,1)} %prefix.1, bf16[2,4096]{1,0:T(2,128)(2,1)} %bitcast.3, bf16[2,1,2,128,1024]{4,3,2,1,0:T(8,128)(2,1)} %suffix.1, s32[256]{0:T(256)} %lengths_in.1, s32[1]{0:T(128)S(6)} %copy.8.slot_in), custom_call_target="tpu_custom_call" | custom-call | tf_op jit(solution)/shard_map/attend/pallas_call | solution.py:390
  48.1 0.6 %copy.7 = bf16[2,1,4096]{2,0,1:T(2,128)(2,1)} copy(bf16[2,1,4096]{2,0,1:T(2,128)(2,1)S(1)} %bitcast.2) | data formatting | bytes 32768

commit v4 on v3

--- a/solution.py
+++ b/solution.py
@@ -19,6 +19,10 @@
 NT = (((1,), (1,)), ((), ()))
 NN = (((1,), (0,)), ((), ()))
 MESH = pl.DeviceIdType.MESH
+OFFSETS = sorted(
+    [(dz, dx, dy) for dz in range(8) for dx in range(4) for dy in range(4) if dz + dx + dy],
+    key=lambda o: -(min(o[0], 8 - o[0]) + min(o[1], 4 - o[1]) + min(o[2], 4 - o[2])))
+FAR, NEAR = OFFSETS[:64], OFFSETS[64:]
 
 
 def dot(a, b, dims):
@@ -53,16 +57,23 @@
             src_ref=src, dst_ref=dst, send_sem=s, recv_sem=r, device_id=dev, device_id_type=MESH)
 
     load_q = pltpu.make_async_copy(queries, qraw, loc_sem.at[9])
+    load_first = pltpu.make_async_copy(prefix.at[0, 0], stage.at[0, 0], loc_sem.at[0])
+    load_first.start()
     load_q.start()
     barrier = pltpu.get_barrier_semaphore()
-    peers = [other]
-    for k in range(1, 16):
-        to = (spot + k) % 16
-        peers.append(at(to // 2, to % 2, z, c))
+    line = (z + 2) % 8
+
+    def mate(k):
+        return (line // 4 * 4 + (line + k) % 4 + 6) % 8
+
+    peers = [other, at(head, 1 - yl, z, c)]
     for k in range(1, 8):
-        peers.append(at(head, yl, (z + k) % 8, c))
+        peers.append(at((head + k) % 8, yl, z, c))
     for k in range(1, 4):
+        peers.append(at(head, yl, zh * 4 + (zl + k) % 4, c))
         peers.append(at(head, 1 - yl, zh * 4 + (zl + k) % 4, c))
+    for k in range(2):
+        peers.append(at(head, yl, (line // 4 * 4 + (line % 4 // 2 * 2 + 2 + k) % 4 + 6) % 8, c))
     for dev in peers:
         pl.semaphore_signal(barrier, inc=1, device_id=dev, device_id_type=MESH)
 
@@ -75,7 +86,6 @@
     load_suf = pltpu.make_async_copy(suffix, suf, loc_sem.at[8])
     load_len = pltpu.make_async_copy(lengths_in, lengths, loc_sem.at[10])
     load_slot = pltpu.make_async_copy(slot_in, slot, loc_sem.at[11])
-    loads[0, 0].start()
     load_suf.start()
     load_len.start()
     load_slot.start()
@@ -91,7 +101,6 @@
         rows = [q32[l:l + 1, (h * GROUP + g) * HD:(h * GROUP + g + 1) * HD]
                 for l in range(2) for g in range(GROUP)]
         qmsg[h] = jnp.concatenate(rows, axis=0).astype(bf16)
-    loads[0, 0].wait()
     pl.semaphore_wait(barrier, len(peers))
 
     for k in range(1, 8):
@@ -122,6 +131,7 @@
 
     full = [(2, 0), (2, 1), (1, 0), (1, 1), (3, 0), (3, 1), (0, 1)]
 
+    load_first.wait()
     kv_send(0, 0, [(2, 0), (2, 1), (0, 1), (1, 0)])
 
     load_suf.wait()
@@ -163,19 +173,19 @@
 
     pairs = [regroup(qa[2 * j].astype(f32), qa[2 * j + 1].astype(f32)) for j in range(4)]
     qall[z, yl] = jnp.concatenate([p[l] for l in range(2) for p in pairs], axis=0).astype(bf16)
-    line = (z + 2) % 8
-
-    def mate(k):
-        return (line // 4 * 4 + (line + k) % 4 + 6) % 8
-
     mirror = zh * 4 + 3 - zl
 
     def b_send(block, z_to, r):
         remote(qall.at[block, yl], qall.at[block, yl], b_sem.at[0], r, at(head, yl, z_to, c)).start()
+
+    def y_send(z_of):
+        block = qall.at[z_of, yl]
+        remote(block, block, y_sem.at[0], y_sem.at[1], at(head, 1 - yl, z, c)).start()
 
     b_send(z, mirror, b_sem.at[2])
     for k in (2, 1, 3):
         b_send(z, mate(k), b_sem.at[1])
+    y_send(z)
     loads[1, 0].wait()
     kv_send(0, 0, [(1, 1), (3, 0), (3, 1)])
     kv_send(1, 0, [(2, 0)])
@@ -185,26 +195,29 @@
 
     m_wait()
     for k in (2, 1, 3):
-        b_send(mirror, mate(k), b_sem.at[1])
+        b_send(mirror, mate(k), b_sem.at[3])
+    y_send(mirror)
     loads[0, 1].wait()
     kv_send(1, 0, full[1:])
     kv_send(0, 1, full[:2])
     kv_wait(0, 0)
     forward(0, 0).start()
 
-    def b_wait():
-        remote(qall.at[0:6, 0], qall.at[0:6, 0], b_sem.at[0], b_sem.at[1]).wait_recv()
-
-    def y_copy(which):
-        return remote(qall.at[:, which], qall.at[:, which], y_sem.at[0], y_sem.at[1],
-                      at(head, 1 - yl, z, c))
+    def b_wait(r):
+        remote(qall.at[0:3, 0], qall.at[0:3, 0], b_sem.at[0], b_sem.at[r]).wait_recv()
 
     def y_wait():
-        y_copy(1 - yl).wait_recv()
-
-    b_wait()
-    y_copy(yl).start()
-    kv_send(0, 1, full[2:])
+        whole = qall.at[:, 1 - yl]
+        remote(whole, whole, y_sem.at[0], y_sem.at[1]).wait_recv()
+
+    b_wait(1)
+    for k in range(1, 4):
+        y_send(mate(k))
+    kv_send(0, 1, full[2:5])
+    b_wait(3)
+    for k in range(1, 4):
+        y_send(mate(k) // 4 * 4 + 3 - mate(k) % 4)
+    kv_send(0, 1, full[5:])
     loads[1, 1].wait()
 
     def weights(l):
@@ -234,26 +247,20 @@
 
         lax.fori_loop(0, 4, rows, 0, unroll=True)
 
-    def partials(l):
-        def ring(j, carry):
-            dz = 4 + (j + 1) // 2 * (1 - 2 * (j % 2))
-            z_to = (z + dz) % 8
-            for i in range(15, -1, -1):
-                spot_to = (spot + i) % 16
-                copy = remote(
-                    osend.at[l, z_to * 16 + spot_to % 2 * 8 + spot_to // 2], orecv.at[l, spot * 8 + z],
-                    c_s.at[l], c_r.at[l], at(spot_to // 2, spot_to % 2, z_to, c))
-                if i:
-                    copy.start()
-                else:
-                    pl.when(dz != 0)(copy.start)
-            return carry
-
-        lax.fori_loop(0, 8, ring, 0)
-        orecv[l, spot * 8 + z] = osend[l, z * 16 + yl * 8 + head]
+    z_at = [(z + d) % 8 for d in range(8)]
+    x_at = [(x + d) % 4 for d in range(4)]
+    y_at = [(y + d) % 4 for d in range(4)]
+
+    def partials(l, offsets):
+        for dz, dx, dy in offsets:
+            z_to, x_to, y_to = z_at[dz], x_at[dx], y_at[dy]
+            dev = ((x_to * 4 + y_to) * 4 + z_to % 4, z_to // 4 * 2 + c)
+            remote(osend.at[l, z_to * 16 + y_to % 2 * 8 + x_to * 2 + y_to // 2],
+                   orecv.at[l, spot * 8 + z], c_s.at[l], c_r.at[l], dev).start()
 
     def store_partials(l, o):
         osend.at[l].reshape(512, HD)[...] = o.astype(bf16)
+        orecv[l, spot * 8 + z] = osend[l, z * 16 + yl * 8 + head]
 
     def values_own(l):
         oacc[l] = dot(wbuf[l, 0], kown[l, 1].reshape(HD, POS), NT)
@@ -325,15 +332,17 @@
         remote(whole, whole, f_s.at[3], f_r.at[3]).wait_recv()
         store_partials(1, (oacc[1] + last_dot(1, koth, second)) * rden[1])
 
+    values_other(0)
     last_first()
     last_copy().start()
     values_first()
-    values_other(0)
-    partials(0)
     last_pieces()
+    partials(0, FAR)
+    values_second()
+    partials(1, FAR)
     sources()
-    values_second()
-    partials(1)
+    partials(1, NEAR)
+    partials(0, NEAR)
 
     def shares():
         remote(grecv.at[0:15], grecv.at[0:15], g_sem.at[0], g_sem.at[1]).wait_recv()
@@ -370,7 +379,7 @@
 
     remote(qa.at[0:7], qa.at[0:7], a_sem.at[0], a_sem.at[1]).wait_send()
     remote(qall.at[0:7, 0], qall.at[0:7, 0], b_sem.at[0], b_sem.at[1]).wait_send()
-    y_copy(yl).wait_send()
+    remote(qall.at[:, yl], qall.at[:, yl], y_sem.at[0], y_sem.at[1]).wait_send()
     last_copy().wait_send()
     remote(kown.at[1, 1, :, :, second], koth.at[1, 1, :, :, second], f_s.at[3], f_r.at[3]).wait_send()
     remote(lrecv.at[0:7], lrecv.at[0:7], l_sem.at[0], l_sem.at[1]).wait_send()
@@ -422,7 +431,7 @@
             pltpu.VMEM((16, 8, HD), f32),
             pltpu.VMEM((2, 16, 4, 8, HD), f32),
             dma((12,)),
-            dma((2,)), dma((3,)), dma((2,)),
+            dma((2,)), dma((4,)), dma((2,)),
             dma((4,)), dma((4,)), dma((8,)),
             dma((5,)), dma((5,)),
             dma((2,)), dma((2,)),

time: 48.9 us -> 47.9 us (0.980)
  Pallas kernels: 47.4 us -> 46.6 us
    pallas_call x1, Pallas kernels: 47.4 us -> 46.6 us  [body(): pl.pallas_call(kernel, out_shape=pltpu.VMEM((2, QH * HD), bf), in_specs=[...]
where the time goes in v4:
time: 47.9 us; the launch traced here: 47.8 us
  Pallas kernels  46.6 us (97%)
  between operations  0.66 us (1%)
  local copies, waits for them, and re-layouts  0.61 us (1%)
    pallas_call x1, Pallas kernels, body(): pl.pallas_call(kernel, out_shape=pltpu.VMEM((2, QH * HD), bf), in_specs=[...  46.6 us

profile of v4, /device:TPU:1, one launch (start us, length us, event | category | flops | bytes accessed | tf_op | source)
XLA Modules:
  0.0 47.8 jit_solution(14381185872863957621)
XLA Ops:
  0.7 46.6 %attend.1 = bf16[2,4096]{1,0:T(2,128)(2,1)S(1)} custom-call(bf16[2,2,16,8192]{3,2,1,0:T(8,128)(2,1)} %prefix.1, bf16[2,4096]{1,0:T(2,128)(2,1)} %bitcast.3, bf16[2,1,2,128,1024]{4,3,2,1,0:T(8,128)(2,1)} %suffix.1, s32[256]{0:T(256)} %lengths_in.1, s32[1]{0:T(128)S(6)} %copy.8.slot_in), custom_call_target="tpu_custom_call" | custom-call | tf_op jit(solution)/shard_map/attend/pallas_call | solution.py:399
  47.2 0.6 %copy.7 = bf16[2,1,4096]{2,0,1:T(2,128)(2,1)} copy(bf16[2,1,4096]{2,0,1:T(2,128)(2,1)S(1)} %bitcast.2) | data formatting | bytes 32768

commit v5 on v4

--- a/solution.py
+++ b/solution.py
@@ -32,7 +32,7 @@
 def kernel(
     prefix, queries, suffix, lengths_in, slot_in, out,
     lengths, slot, stage, kown, koth, suf, qraw, qmsg, qa, qall, wbuf, rden, oacc, sbuf_o, sbuf_l,
-    osend, orecv, lsend, lrecv, gsend, grecv, share,
+    osend, orecv, lsend, hsend, lrecv, gsend, grecv, lfin, share,
     loc_sem, a_sem, b_sem, y_sem, kv_s, kv_r, v1_r, f_s, f_r, c_s, c_r, l_sem, g_sem,
 ):
     f32, bf16 = jnp.float32, jnp.bfloat16
@@ -79,7 +79,7 @@
 
     order = ((0, 0), (1, 0), (0, 1), (1, 1))
     loads = {(l, k): pltpu.make_async_copy(prefix.at[l, k], stage.at[l, k], loc_sem.at[l * 2 + k])
-             for l, k in order}
+             for l, k in order[1:]}
     owns = {(l, k): pltpu.make_async_copy(
         prefix.at[l, k, :, pl.ds(pl.multiple_of(part * POS, POS), POS)],
         kown.at[l, k, part], loc_sem.at[4 + l * 2 + k]) for l, k in order}
@@ -270,8 +270,7 @@
         store_partials(l, (oacc[l] + dot(wbuf[l, 1], koth[l, 1].reshape(HD, POS), NT)) * rden[l])
 
     def sources():
-        remote(lrecv.at[0:7], lrecv.at[0:7], l_sem.at[0], l_sem.at[1]).wait_recv()
-        ls = jnp.concatenate([lrecv[...].reshape(8, HD), jnp.full((120, HD), NEG, f32)], axis=0).T
+        ls = jnp.concatenate([lsend[...].reshape(8, HD), jnp.full((120, HD), NEG, f32)], axis=0).T
         for half in range(2):
             for j in range(4):
                 base = half * 32 + j * 8
@@ -284,6 +283,14 @@
                    at(to // 2, to % 2, z, c)).start()
         grecv[spot] = gsend[spot]
 
+    def columns():
+        remote(grecv.at[0:15], grecv.at[0:15], g_sem.at[0], g_sem.at[1]).wait_recv()
+        hsend[...] = grecv[...].reshape(128, HD).T[:8].reshape(8, 1, HD)
+        for k in (4, 3, 5, 2, 6, 1, 7):
+            to = (z + k) % 8
+            remote(hsend.at[to], lrecv.at[z], l_sem.at[0], l_sem.at[1], at(head, yl, to, c)).start()
+        lrecv[z] = hsend[z]
+
     kv_wait(1, 0)
     forward(1, 0).start()
     kv_send(1, 1, full, 0)
@@ -291,10 +298,7 @@
     weights(0)
     kv_send(1, 1, full, 1)
     weights(1)
-    for k in range(1, 8):
-        to = (z + k) % 8
-        remote(lsend.at[to], lrecv.at[z], l_sem.at[0], l_sem.at[1], at(head, yl, to, c)).start()
-    lrecv[z] = lsend[z]
+    sources()
     kv_wait(0, 1)
     forward(0, 1).start()
     values_own(0)
@@ -328,27 +332,29 @@
         oacc[1] = oacc[1] + last_dot(0, kown, second)
         last_copy().wait_recv()
         oacc[1] = oacc[1] + last_dot(1, koth, first)
+        columns()
         whole = koth.at[1, 1, :, :, second]
         remote(whole, whole, f_s.at[3], f_r.at[3]).wait_recv()
         store_partials(1, (oacc[1] + last_dot(1, koth, second)) * rden[1])
 
     values_other(0)
+    partials(0, FAR)
     last_first()
     last_copy().start()
     values_first()
     last_pieces()
-    partials(0, FAR)
     values_second()
     partials(1, FAR)
-    sources()
     partials(1, NEAR)
     partials(0, NEAR)
 
     def shares():
-        remote(grecv.at[0:15], grecv.at[0:15], g_sem.at[0], g_sem.at[1]).wait_recv()
+        remote(lrecv.at[0:7], lrecv.at[0:7], l_sem.at[0], l_sem.at[1]).wait_recv()
+        ls = jnp.concatenate([lrecv[...].reshape(8, HD), jnp.full((120, HD), NEG, f32)], axis=0).T
+        lfin[...] = ls.reshape(16, 8, HD)
 
         def one_head(h, carry):
-            la, lb, lc = grecv[2 * h], grecv[2 * h + 1], sbuf_l[h]
+            la, lb, lc = lfin[2 * h], lfin[2 * h + 1], sbuf_l[h]
             top = jnp.max(jnp.maximum(jnp.maximum(la, lb), lc), axis=1, keepdims=True)
             a, b, s = jnp.exp2(la - top), jnp.exp2(lb - top), jnp.exp2(lc - top)
             den = jnp.sum(a + b, axis=1, keepdims=True) + s
@@ -427,6 +433,8 @@
             pltpu.VMEM((2, 128, GROUP, HD), bf),
             pltpu.VMEM((8, 1, HD), f32),
             pltpu.VMEM((8, 1, HD), f32),
+            pltpu.VMEM((8, 1, HD), f32),
+            pltpu.VMEM((16, 8, HD), f32),
             pltpu.VMEM((16, 8, HD), f32),
             pltpu.VMEM((16, 8, HD), f32),
             pltpu.VMEM((2, 16, 4, 8, HD), f32),

time: 47.9 us -> 47.7 us (level)
  no operation moved by 1% of the time
where the time goes in v5:
time: 47.7 us; the launch traced here: 47.6 us
  Pallas kernels  46.3 us (97%)
  between operations  0.66 us (1%)
  local copies, waits for them, and re-layouts  0.61 us (1%)
    pallas_call x1, Pallas kernels, body(): pl.pallas_call(kernel, out_shape=pltpu.VMEM((2, QH * HD), bf), in_specs=[...  46.3 us

profile of v5, /device:TPU:1, one launch (start us, length us, event | category | flops | bytes accessed | tf_op | source)
XLA Modules:
  0.0 47.6 jit_solution(6692085629930977543)
XLA Ops:
  0.7 46.3 %attend.1 = bf16[2,4096]{1,0:T(2,128)(2,1)S(1)} custom-call(bf16[2,2,16,8192]{3,2,1,0:T(8,128)(2,1)} %prefix.1, bf16[2,4096]{1,0:T(2,128)(2,1)} %bitcast.3, bf16[2,1,2,128,1024]{4,3,2,1,0:T(8,128)(2,1)} %suffix.1, s32[256]{0:T(256)} %lengths_in.1, s32[1]{0:T(128)S(6)} %copy.8.slot_in), custom_call_target="tpu_custom_call" | custom-call | tf_op jit(solution)/shard_map/attend/pallas_call | solution.py:405
  47.0 0.6 %copy.7 = bf16[2,1,4096]{2,0,1:T(2,128)(2,1)} copy(bf16[2,1,4096]{2,0,1:T(2,128)(2,1)S(1)} %bitcast.2) | data formatting | bytes 32768

commit v6 on v5

--- a/solution.py
+++ b/solution.py
@@ -129,10 +129,11 @@
     def forward(l, k):
         return remote(kown.at[l, k], koth.at[l, k], f_s.at[l * 2 + k], f_r.at[l * 2 + k])
 
-    full = [(2, 0), (2, 1), (1, 0), (1, 1), (3, 0), (3, 1), (0, 1)]
+    to_mirror, to_next = 3 - 2 * (zl % 2), 1 + 2 * (zl % 2)
+    full = [(to_mirror, 0), (to_mirror, 1), (2, 0), (2, 1), (to_next, 0), (to_next, 1), (0, 1)]
 
     load_first.wait()
-    kv_send(0, 0, [(2, 0), (2, 1), (0, 1), (1, 0)])
+    kv_send(0, 0, full[:3] + full[6:])
 
     load_suf.wait()
     load_len.wait()
@@ -187,8 +188,8 @@
         b_send(z, mate(k), b_sem.at[1])
     y_send(z)
     loads[1, 0].wait()
-    kv_send(0, 0, [(1, 1), (3, 0), (3, 1)])
-    kv_send(1, 0, [(2, 0)])
+    kv_send(0, 0, full[3:6])
+    kv_send(1, 0, full[:1])
 
     def m_wait():
         remote(qall.at[mirror, yl], qall.at[mirror, yl], b_sem.at[0], b_sem.at[2]).wait_recv()
@@ -323,7 +324,7 @@
         own = kown.at[1, 1, part, :, second]
         remote(own, koth.at[1, 1, part, :, second], f_s.at[3], f_r.at[3]).start()
         for dz, dy in full:
-            src = (yl + dy) % 2 * 4 + (zl + 4 - dz) % 4
+            src = (yl + dy) % 2 * 4 + (zl + dz) % 4
             piece = kown.at[1, 1, src, :, second]
             remote(piece, piece, kv_s.at[0], v1_r.at[src]).wait_recv()
             remote(piece, koth.at[1, 1, src, :, second], f_s.at[3], f_r.at[3]).start()

time: 47.7 us -> 47.5 us (level)
  no operation moved by 1% of the time
where the time goes in v6:
time: 47.5 us; the launch traced here: 47.4 us
  Pallas kernels  46.1 us (97%)
  between operations  0.66 us (1%)
  local copies, waits for them, and re-layouts  0.61 us (1%)
    pallas_call x1, Pallas kernels, body(): pl.pallas_call(kernel, out_shape=pltpu.VMEM((2, QH * HD), bf), in_specs=[...  46.1 us

profile of v6, /device:TPU:1, one launch (start us, length us, event | category | flops | bytes accessed | tf_op | source)
XLA Modules:
  0.0 47.4 jit_solution(16126160922407405484)
XLA Ops:
  0.7 46.1 %attend.1 = bf16[2,4096]{1,0:T(2,128)(2,1)S(1)} custom-call(bf16[2,2,16,8192]{3,2,1,0:T(8,128)(2,1)} %prefix.1, bf16[2,4096]{1,0:T(2,128)(2,1)} %bitcast.3, bf16[2,1,2,128,1024]{4,3,2,1,0:T(8,128)(2,1)} %suffix.1, s32[256]{0:T(256)} %lengths_in.1, s32[1]{0:T(128)S(6)} %copy.8.slot_in), custom_call_target="tpu_custom_call" | custom-call | tf_op jit(solution)/shard_map/attend/pallas_call | solution.py:406
  46.8 0.6 %copy.7 = bf16[2,1,4096]{2,0,1:T(2,128)(2,1)} copy(bf16[2,1,4096]{2,0,1:T(2,128)(2,1)S(1)} %bitcast.2) | data formatting | bytes 32768

commit v7 on v6

--- a/solution.py
+++ b/solution.py
@@ -344,10 +344,10 @@
     last_copy().start()
     values_first()
     last_pieces()
+    partials(0, NEAR)
     values_second()
     partials(1, FAR)
     partials(1, NEAR)
-    partials(0, NEAR)
 
     def shares():
         remote(lrecv.at[0:7], lrecv.at[0:7], l_sem.at[0], l_sem.at[1]).wait_recv()

time: 47.5 us -> 48 us (1.011)
  Pallas kernels: 46.1 us -> 46.6 us
    pallas_call x1, Pallas kernels: 46.1 us -> 46.6 us  [body(): pl.pallas_call(kernel, out_shape=pltpu.VMEM((2, QH * HD), bf), in_specs=[...]
where the time goes in v7:
time: 48 us; the launch traced here: 47.9 us
  Pallas kernels  46.6 us (97%)
  between operations  0.66 us (1%)
  local copies, waits for them, and re-layouts  0.61 us (1%)
    pallas_call x1, Pallas kernels, body(): pl.pallas_call(kernel, out_shape=pltpu.VMEM((2, QH * HD), bf), in_specs=[...  46.6 us

profile of v7, /device:TPU:1, one launch (start us, length us, event | category | flops | bytes accessed | tf_op | source)
XLA Modules:
  0.0 47.9 jit_solution(13367555427355911638)
XLA Ops:
  0.7 46.6 %attend.1 = bf16[2,4096]{1,0:T(2,128)(2,1)S(1)} custom-call(bf16[2,2,16,8192]{3,2,1,0:T(8,128)(2,1)} %prefix.1, bf16[2,4096]{1,0:T(2,128)(2,1)} %bitcast.3, bf16[2,1,2,128,1024]{4,3,2,1,0:T(8,128)(2,1)} %suffix.1, s32[256]{0:T(256)} %lengths_in.1, s32[1]{0:T(128)S(6)} %copy.8.slot_in), custom_call_target="tpu_custom_call" | custom-call | tf_op jit(solution)/shard_map/attend/pallas_call | solution.py:406
  47.3 0.6 %copy.7 = bf16[2,1,4096]{2,0,1:T(2,128)(2,1)} copy(bf16[2,1,4096]{2,0,1:T(2,128)(2,1)S(1)} %bitcast.2) | data formatting | bytes 32768

commit v8 on v6

--- a/solution.py
+++ b/solution.py
@@ -15,7 +15,7 @@
 NEG = -1e30
 SCALE2 = HD ** -0.5 * math.log2(math.e)
 POS = 1024
-HALF = POS // 2
+LAST = POS // 4
 NT = (((1,), (1,)), ((), ()))
 NN = (((1,), (0,)), ((), ()))
 MESH = pl.DeviceIdType.MESH
@@ -115,11 +115,11 @@
             if half is None:
                 start, size, dst, r = 0, POS, kown.at[l, k, part], kv_r.at[l * 2 + k]
             else:
-                start, size = half * HALF, HALF
-                dst = kown.at[l, k, part, :, start:start + HALF]
+                start, size = (POS - LAST, LAST) if half else (0, POS - LAST)
+                dst = kown.at[l, k, part, :, start:start + size]
                 r = v1_r.at[part] if half else kv_r.at[l * 2 + k]
             remote(
-                stage.at[l, k, :, pl.ds(pl.multiple_of(to * POS + start, HALF), size)],
+                stage.at[l, k, :, pl.ds(pl.multiple_of(to * POS + start, LAST), size)],
                 dst, kv_s.at[l * 2 + k], r, at(head, yl_to, zh * 4 + zl_to, c)).start()
 
     def kv_wait(l, k):
@@ -304,7 +304,7 @@
     forward(0, 1).start()
     values_own(0)
 
-    first, second = slice(0, HALF), slice(HALF, POS)
+    first, second = slice(0, POS - LAST), slice(POS - LAST, POS)
 
     def last_first():
         owns[1, 1].wait()
@@ -315,7 +315,7 @@
         return remote(kown.at[1, 1, :, :, first], koth.at[1, 1, :, :, first], f_s.at[4], f_r.at[4])
 
     def last_dot(which, ref, span):
-        return dot(wbuf[1, which, :, span], ref[1, 1, :, :, span].reshape(HD, HALF), NT)
+        return dot(wbuf[1, which, :, span], ref[1, 1, :, :, span].reshape(HD, span.stop - span.start), NT)
 
     def values_first():
         oacc[1] = last_dot(0, kown, first)

time: 47.5 us -> 47.4 us (level)
  no operation moved by 1% of the time
where the time goes in v8:
time: 47.4 us; the launch traced here: 47.3 us
  Pallas kernels  46 us (97%)
  between operations  0.66 us (1%)
  local copies, waits for them, and re-layouts  0.61 us (1%)
    pallas_call x1, Pallas kernels, body(): pl.pallas_call(kernel, out_shape=pltpu.VMEM((2, QH * HD), bf), in_specs=[...  46 us

profile of v8, /device:TPU:1, one launch (start us, length us, event | category | flops | bytes accessed | tf_op | source)
XLA Modules:
  0.0 47.3 jit_solution(946842603095198993)
XLA Ops:
  0.7 46.0 %attend.1 = bf16[2,4096]{1,0:T(2,128)(2,1)S(1)} custom-call(bf16[2,2,16,8192]{3,2,1,0:T(8,128)(2,1)} %prefix.1, bf16[2,4096]{1,0:T(2,128)(2,1)} %bitcast.3, bf16[2,1,2,128,1024]{4,3,2,1,0:T(8,128)(2,1)} %suffix.1, s32[256]{0:T(256)} %lengths_in.1, s32[1]{0:T(128)S(6)} %copy.8.slot_in), custom_call_target="tpu_custom_call" | custom-call | tf_op jit(solution)/shard_map/attend/pallas_call | solution.py:406
  46.7 0.6 %copy.7 = bf16[2,1,4096]{2,0,1:T(2,128)(2,1)} copy(bf16[2,1,4096]{2,0,1:T(2,128)(2,1)S(1)} %bitcast.2) | data formatting | bytes 32768
